TPU v7x, 128 devices: a whole 4x4x4 slice. The times are simulated.
128 devices in a mesh: wa: 32 (over x, z_hi, y), ch: 4 (over z_lo, core).
Axes of the slice: x: 4, y: 4, z: 4 (z_hi: 2, z_lo: 2; z = z_hi * 2 + z_lo), core: 2. Of those that a mesh axis runs over, the one named last changes fastest.
Arguments:
- grid_cells: int32 [2, 65536], P(None, ('wa', 'ch')), may hold values from -4096 to 4095
- visibilities: float32 [2, 65536], P(None, ('wa', 'ch')), may hold values from -6 to 6
- weights: float32 [65536], P(('wa', 'ch')), may hold values from 0.25 to 4
- layer_index: int32 [65536], P(('wa', 'ch')), may hold values from 0 to 31, as said below
- group_index: int32 [65536], P(('wa', 'ch')), may hold values from 0 to 3, as said below
- plane_depths: float32 [32], P('wa'), may hold values from -1000 to 1000
- sky_model: float32 [4, 512, 4096], P('ch', 'wa'), may hold values from -6 to 6
Outputs:
- residual: float32 [4, 512, 4096], P('ch', 'wa')
Inputs may be any that keep to these rules, and one draw needn't show every extreme that they name: `layer_index`: among the 512 visibilities of one device, at most 8 have the same layer and the same group; one layer and group has exactly 8 on every device. `group_index`: drawn together with layer_index.
All inputs are finite; a program needn't handle non-finite values.
Results may differ from a plain program's by a relative error of at most 0.0026.
Values sent between devices are 32-bit elements; how exact they have to be, the bound alone decides.
A program may use at most 128 MiB of HBM per device.

v0:
```python
import math

import jax
import jax.numpy as jnp
from jax import lax
from jax.sharding import Mesh
from jax.sharding import PartitionSpec as P

GRID = 8192
WA = ("wa_0", "wa_1", "wa_2")
CH = ("ch_0", "ch_1")
WA_CH = ("wa_0", "wa_1", "wa_2", "ch_0", "ch_1")


def in_blocks(array, dim, peers):
    before, after = (array.shape[:dim], array.shape[dim + 1 :])
    return jnp.moveaxis(array.reshape(*before, peers, -1, *after), dim, 0)


def joined_along(parts, dim):
    parts = jnp.moveaxis(parts, 0, dim)
    shape = parts.shape
    return parts.reshape(*shape[:dim], shape[dim] * shape[dim + 1], *shape[dim + 2 :])


def one_exchange(array, axis, axes, splits, concats):
    sizes = [lax.axis_size(a) for a in axes]
    parts = in_blocks(array, splits[0], sizes[0])
    parts = jnp.moveaxis(in_blocks(parts, splits[1] + 1, sizes[1]), 0, 1)
    inside = parts.shape[2:]
    parts = parts.reshape(-1, *inside)
    parts = lax.all_to_all(parts, axis, split_axis=0, concat_axis=0, tiled=True)
    parts = joined_along(parts.reshape(*sizes, *inside), concats[0] + 1)
    return joined_along(parts, concats[1])


def over_axes(array, axes):
    for axis in axes:
        array = lax.psum(array, axis)
    return array


def phase_table(left, right, grid_size):
    product = jnp.mod(left[:, None] * right[None, :], grid_size)
    return product.astype(jnp.float32) * (2.0 * math.pi / grid_size)


def column_factor(real_part, imag_part, weight, column_cells, columns, grid_size):
    pixels = jnp.arange(columns, dtype=jnp.int32) - columns // 2 + grid_size // 8
    angles = phase_table(column_cells, pixels, grid_size)
    weighted_real = weight * real_part
    weighted_imag = weight * imag_part
    cosines = jnp.cos(angles)
    sine_values = jnp.sin(angles)
    column_real = (weighted_real[:, None] * cosines - weighted_imag[:, None] * sine_values).astype(
        jnp.bfloat16
    )
    column_imag = (weighted_real[:, None] * sine_values + weighted_imag[:, None] * cosines).astype(
        jnp.bfloat16
    )
    return jnp.concatenate([column_real, column_imag], 0)


def row_factor(row_cells, row_count, total_rows, grid_size):
    pixels = jnp.arange(row_count, dtype=jnp.int32) - total_rows // 2 + grid_size // 8
    angles = phase_table(pixels, row_cells, grid_size)
    real_part = jnp.cos(angles).astype(jnp.bfloat16)
    imag_part = jnp.sin(angles).astype(jnp.bfloat16)
    upper_half = jnp.concatenate([real_part, -imag_part], 1)
    lower_half = jnp.concatenate([imag_part, real_part], 1)
    return jnp.concatenate([upper_half, lower_half], 0)


def layer_image(row_factors, column_factors, w_value, row_count, total_rows, columns, grid_size):
    product = jnp.dot(row_factors, column_factors, preferred_element_type=jnp.float32)
    real_sum = product[:row_count]
    imag_sum = product[row_count:]
    row_pixels = jnp.arange(row_count, dtype=jnp.int32) - total_rows // 2 + grid_size // 8
    column_pixels = jnp.arange(columns, dtype=jnp.int32) - columns // 2 + grid_size // 8
    row_cosine = 0.8 * row_pixels.astype(jnp.float32) / grid_size
    column_cosine = 0.8 * column_pixels.astype(jnp.float32) / grid_size
    depth_term = jnp.sqrt(1.0 - row_cosine[:, None] ** 2 - column_cosine[None, :] ** 2) - 1.0
    screen = 2.0 * math.pi * w_value * depth_term
    return jnp.cos(screen) * real_sum - jnp.sin(screen) * imag_sum


def on_device(grid_cells, visibilities, weights, layer_index, group_index, plane_depths, sky_model):
    layer_count = lax.axis_size(WA)
    groups = lax.axis_size(CH)
    dest_count = layer_count * groups
    held = weights.shape[0]
    capacity = 2 * held // dest_count
    rows_dev = sky_model.shape[1]
    columns = sky_model.shape[2]
    total_rows = rows_dev * layer_count
    target = layer_index * groups + group_index
    onehot = (target[:, None] == jnp.arange(dest_count, dtype=jnp.int32)[None, :]).astype(jnp.int32)
    before = jnp.cumsum(onehot, 0) - onehot
    slot_rank = jnp.sum(before * onehot, 1)
    slot_index = target * capacity + slot_rank
    payload = jnp.stack(
        [
            visibilities[0],
            visibilities[1],
            weights,
            grid_cells[0].astype(jnp.float32),
            grid_cells[1].astype(jnp.float32),
        ],
        0,
    )
    outgoing = jnp.zeros((5, dest_count * capacity), jnp.float32).at[:, slot_index].set(payload)
    arrived = one_exchange(
        outgoing.reshape(5, layer_count, groups, capacity), WA_CH, (WA, CH), (1, 2), (1, 2)
    )
    received = arrived.reshape(5, dest_count * capacity)
    squares = weights * weights
    member = (group_index[None, :] == jnp.arange(groups, dtype=jnp.int32)[:, None]).astype(
        jnp.float32
    )
    per_group = jnp.sum(member * squares[None, :], 1)
    totals = over_axes(per_group, WA_CH)
    picked = (jnp.arange(groups, dtype=jnp.int32) == lax.axis_index(CH)).astype(jnp.float32)
    noise_power = jnp.sum(totals * picked)
    row_cells = received[3].astype(jnp.int32)
    column_cells = received[4].astype(jnp.int32)
    column_factors = column_factor(
        received[0], received[1], received[2], column_cells, columns, GRID
    )
    row_factors = row_factor(row_cells, rows_dev * lax.axis_size(WA), total_rows, GRID)
    dirty_tile = lax.psum_scatter(
        layer_image(
            row_factors,
            column_factors,
            plane_depths[0],
            rows_dev * lax.axis_size(WA),
            total_rows,
            columns,
            GRID,
        ),
        WA,
        scatter_dimension=0,
        tiled=True,
    )
    return (dirty_tile * lax.rsqrt(noise_power) - sky_model[0])[None]


def solution(mesh):
    finer = Mesh(mesh.devices.reshape(4, 2, 4, 2, 2), ("wa_0", "wa_1", "wa_2", "ch_0", "ch_1"))
    return jax.shard_map(
        on_device,
        mesh=finer,
        in_specs=(
            P(None, WA_CH),
            P(None, WA_CH),
            P(WA_CH),
            P(WA_CH),
            P(WA_CH),
            P(WA),
            P(CH, WA, None),
        ),
        out_specs=P(CH, WA, None),
        check_vma=False,
    )
```

profile of v0, /device:TPU:0, one launch (start us, length us, event | category | flops | bytes accessed | tf_op | source)
XLA Modules:
  0.0 395.7 jit_solution(4165244337827797568)
XLA Ops:
  6.5 0.7 multiply_add_fusion
  7.2 0.1 copy.23
  7.4 0.2 fusion.23
  7.7 0.2 fusion.21
  7.9 0.8 slice_convert_fusion.3
  8.7 0.7 maximum_bitcast_fusion
  9.4 0.1 copy.25
  9.6 1.8 scatter_custom_fusion
  11.4 1.5 copy.26
  12.9 11.2 %all-to-all-start = ((f32[128,5,1,1,8]{4,3,2,1,0:T(1,128)}), f32[128,5,1,1,8]{4,3,2,1,0:T(1,128)S(1)}, u32[]{:S(2)}, u32[]{:S(2)}) async-start(f32[128,5,1,1,8]{4,3,2,1,0:T(1,128)} %bitcast.11), calls=%async_computation | async-start | bytes 655360 | tf_op jit(solution)/shard_map/all_to_all | solution.py:32
  24.1 0.0 reduce-scatter.2.cloned.1.call-start
  24.9 10.6 %all-to-all-done = f32[128,5,1,1,8]{4,3,2,1,0:T(1,128)S(1)} async-done(((f32[128,5,1,1,8]{4,3,2,1,0:T(1,128)}), f32[128,5,1,1,8]{4,3,2,1,0:T(1,128)S(1)}, u32[]{:S(2)}, u32[]{:S(2)}) %all-to-all-start) | async-done | bytes 20512 | tf_op jit(solution)/shard_map/all_to_all | solution.py:32
  35.5 0.1 copy.29
  35.6 0.1 slice_convert_fusion.1
  35.6 0.1 convert_element_type.76
  35.8 8.9 %sine_convert_fusion = (bf16[512,1024]{1,0:T(8,128)(2,1)S(1)}, bf16[512,1024]{1,0:T(8,128)(2,1)S(1)}) fusion(s32[1024]{0:T(1024)S(1)} %convert_element_type.76, s32[512]{0:T(512)S(1)} %iota_add_fusion.1), kind=kLoop, calls=%fused_computation.35 | loop fusion | flops 8388608 | bytes 2103296 | tf_op jit(solution)/shard_map/convert_element_type | solution.py:68
  44.7 8.4 %fusion.27 = bf16[512,1024]{1,0:T(8,128)(2,1)S(1)} fusion(s32[1024]{0:T(1024)S(1)} %convert_element_type.76, s32[512]{0:T(512)S(1)} %iota_add_fusion.1), kind=kLoop, calls=%fused_computation.49 | loop fusion | flops 9437184 | bytes 1054720 | tf_op jit(solution)/shard_map/neg | solution.py:69
  53.2 0.1 convert_element_type.81
  53.3 0.1 mul.155
  53.4 0.1 mul.164
  53.5 71.8 %subtract_convert_fusion = (bf16[1024,4096]{1,0:T(8,128)(2,1)}, bf16[1024,4096]{1,0:T(8,128)(2,1)}) fusion(f32[1024]{0:T(1024)S(1)} %mul.164, s32[4096]{0:T(1024)S(1)} %iota_add_fusion, s32[1024]{0:T(1024)S(1)} %convert_element_type.81, f32[1024]{0:T(1024)S(1)} %mul.155), kind=kLoop, calls=%fused_computation.14 | loop fusion | flops 92274688 | bytes 16805888 | tf_op jit(solution)/shard_map/convert_element_type | solution.py:55
  125.2 24.5 %fusion.3 = f32[1024,4096]{1,0:T(8,128)} fusion(bf16[1024,4096]{1,0:T(8,128)(2,1)} %get-tuple-element.10, bf16[1024,4096]{1,0:T(8,128)(2,1)} %get-tuple-element.9, bf16[512,1024]{1,0:T(8,128)(2,1)S(1)} %get-tuple-element.12, bf16[512,1024]{1,0:T(8,128)(2,1)S(1)} %get-tuple-element.11, bf16[512,1024]{1,0:T(8,128)(2,1)S(1)} %fusion.27), kind=kOutput, calls=%fused_computation.9 | convolution fusion | flops 17230200832 | bytes 36700160 | tf_op jit(solution)/shard_map/dot_general | solution.py:75
  149.7 35.9 %fusion.7 = f32[512,4096]{1,0:T(8,128)} fusion(f32[1024,4096]{1,0:T(8,128)} %fusion.3, f32[4096]{0:T(1024)S(1)} %multiply_multiply_fusion, f32[512]{0:T(512)S(1)} %multiply_subtract_fusion, f32[]{:T(128)} %bitcast), kind=kLoop, calls=%fused_computation.16 | loop fusion | flops 12582912 | bytes 25184260 | tf_op jit(solution)/shard_map/sub | solution.py:84
  185.6 0.0 copy-start.1
  185.6 0.0 copy-start.2
  185.6 0.0 copy-start
  185.7 0.0 reduce-scatter.2.cloned.1.call-update
  185.7 0.6 copy-done.1
  186.3 0.0 copy-done.2
  186.3 0.1 select_reduce_fusion
  186.4 8.9 %psum.35 = f32[4]{0:T(128)S(1)} all-reduce(f32[4]{0:T(128)S(1)} %select_reduce_fusion), channel_id=1, replica_groups=mesh['wa_0'=4,'wa_1'=2,'wa_2'=4,'ch_0'=2,'ch_1'=2] {'wa_0'}, use_global_device_ids=true, to_apply=%region_6.7 | all-reduce | flops 4 | bytes 32 | tf_op jit(solution)/shard_map/psum | solution.py:39
  195.3 6.4 %psum.36 = f32[4]{0:T(128)S(1)} all-reduce(f32[4]{0:T(128)S(1)} %psum.35), channel_id=1, replica_groups=mesh['wa_0'=4,'wa_1'=2,'wa_2'=4,'ch_0'=2,'ch_1'=2] {'wa_1'}, use_global_device_ids=true, to_apply=%region_7.8 | all-reduce | flops 4 | bytes 32 | tf_op jit(solution)/shard_map/psum | solution.py:39
  201.7 9.4 %psum.37 = f32[4]{0:T(128)S(1)} all-reduce(f32[4]{0:T(128)S(1)} %psum.36), channel_id=1, replica_groups=mesh['wa_0'=4,'wa_1'=2,'wa_2'=4,'ch_0'=2,'ch_1'=2] {'wa_2'}, use_global_device_ids=true, to_apply=%region_8.9 | all-reduce | flops 4 | bytes 32 | tf_op jit(solution)/shard_map/psum | solution.py:39
  211.1 5.3 %psum.38 = f32[4]{0:T(128)S(1)} all-reduce(f32[4]{0:T(128)S(1)} %psum.37), channel_id=1, replica_groups=mesh['wa_0'=4,'wa_1'=2,'wa_2'=4,'ch_0'=2,'ch_1'=2] {'ch_0'}, use_global_device_ids=true, to_apply=%region_9.10 | all-reduce | flops 4 | bytes 32 | tf_op jit(solution)/shard_map/psum | solution.py:39
  216.4 2.4 psum.39
  218.9 0.6 fusion.29
  220.2 167.0 %reduce-scatter.2.cloned.1.call-done = f32[16,4096]{1,0:T(8,128)} async-done(((f32[512,4096]{1,0:T(8,128)}), f32[16,4096]{1,0:T(8,128)}) %reduce-scatter.2.cloned.1.call-update) | async-done | bytes 262160 | tf_op jit(solution)/shard_map/reduce_scatter | solution.py:130
  387.1 0.0 copy-done
  387.1 1.7 fusion.22
  (12 shorter events, 0.1 us)
Async XLA Ops:
  12.9 22.6 %all-to-all-start = ((f32[128,5,1,1,8]{4,3,2,1,0:T(1,128)}), f32[128,5,1,1,8]{4,3,2,1,0:T(1,128)S(1)}, u32[]{:S(2)}, u32[]{:S(2)}) async-start(f32[128,5,1,1,8]{4,3,2,1,0:T(1,128)} %bitcast.11), calls=%async_computation | async-start | bytes 655360 | tf_op jit(solution)/shard_map/all_to_all | solution.py:32
  24.1 363.0 %reduce-scatter.2.cloned.1.call-start = ((), (), s32[]{:S(2)}) async-start(), calls=%async_computation.2 | async-start | bytes 8650752 | tf_op jit(solution)/shard_map/reduce_scatter | solution.py:130
  185.6 0.7 copy-start.1
  185.6 0.7 copy-start.2
  185.6 201.5 %copy-start = (f32[1,16,4096]{2,1,0:T(8,128)S(1)}, f32[1,16,4096]{2,1,0:T(8,128)}, u32[]{:S(2)}) copy-start(f32[1,16,4096]{2,1,0:T(8,128)} %param.13) | copy-start | bytes 786436
Sparse Core Ops, SparseCore 0:
  185.8 201.2 reduce-scatter.1
where the time goes:
time: 396 us
  waiting for transfers between devices  178 us (45%)
  other arithmetic  130 us (33%)
  blocking collectives  32.5 us (8%)
  matrix products  24.5 us (6%)
  between operations  14.9 us (4%)
  starting transfers between devices  11.2 us (3%)
  local copies, waits for them, and re-layouts  4.84 us (1%)
    reduce_scatter x1, waiting for transfers between devices, on_device(): lax.psum_scatter(layer_image(row_factors, column_factors, plane_depths[0]...  167 us
    convert_element_type x1, other arithmetic, column_factor(): (weighted_real[:, None] * cosines - weighted_imag[:, None] * sine_values)...  71.8 us
    sub x1, other arithmetic, layer_image(): return jnp.cos(screen) * real_sum - jnp.sin(screen) * imag_sum  35.9 us
    psum x5, blocking collectives, over_axes(): array = lax.psum(array, axis)  32.5 us
    dot_general x1, matrix products, layer_image(): jnp.dot(row_factors, column_factors, preferred_element_type=jnp.float32)  24.5 us
    all_to_all x1, starting transfers between devices, one_exchange(): parts = lax.all_to_all(parts, axis, split_axis=0, concat_axis=0, tiled=True)  11.2 us
    all_to_all x1, waiting for transfers between devices, one_exchange(): parts = lax.all_to_all(parts, axis, split_axis=0, concat_axis=0, tiled=True)  10.6 us
    convert_element_type x1, other arithmetic, row_factor(): imag_part = jnp.sin(angles).astype(jnp.bfloat16)  8.95 us
  transfers between devices with their start and end apart: 2, of which 2 were waited for; matrix products, arithmetic and copies ran while one was open for 0% of the time, Pallas kernels for 0%

commit v1 on v0

v1 whole, which is shorter than its diff:
```python
import functools
import math

import jax
import jax.numpy as jnp
from jax import lax
from jax.experimental import pallas as pl
from jax.experimental.pallas import tpu as pltpu
from jax.sharding import PartitionSpec as P

F32 = jnp.float32
BF16 = jnp.bfloat16
I32 = jnp.int32

GRID = 8192
LAYERS = 32
GROUPS = 4
SOURCES = 128
CAP = 8
LANES = 128
VIS_DEV = 512
ROWS = 16
COLS = 4096
BLOCKS = COLS // 256
MSG = 10

SIN_C = (4.442882919124344, -7.308245686509099, 3.6063542184331383, -0.8461116503741475, 0.10982451642439378)
COS_C = (1.4142134962552289, -6.978850948563853, 5.7394603769076955, -1.8835579059892091, 0.31068802753070307)


def horner(g, coefs):
    total = coefs[-1] * g + coefs[-2]
    for c in coefs[-3::-1]:
        total = total * g + c
    return total


def sincos_turns(f):
    g = f * f
    s = horner(g, SIN_C) * f
    c = horner(g, COS_C)
    return 1.0 - s * s, s * c


def sincos_phase(p):
    q = ((p + GRID) & (2 * GRID - 1)) - GRID
    return sincos_turns(q.astype(F32) * (1.0 / (2 * GRID)))


def cmul(a, b):
    return a[0] * b[0] - a[1] * b[1], a[0] * b[1] + a[1] * b[0]


def route_kernel(cells, vis, weights, layer, group, depth, out):
    w = weights[...]
    target_row = (layer[...] * GROUPS + group[...]).astype(F32)
    blocks = VIS_DEV // LANES
    lane = lax.broadcasted_iota(I32, (LANES, LANES), 1)
    sub = lax.broadcasted_iota(I32, (LANES, LANES), 0)
    slots = []
    for b in range(blocks):
        mine = target_row[:, b * LANES : (b + 1) * LANES]
        across = jnp.broadcast_to(mine, (LANES, LANES)).T
        hits = jnp.where((across == mine) & (lane < sub), 1.0, 0.0)
        for other in range(b):
            theirs = target_row[:, other * LANES : (other + 1) * LANES]
            hits += jnp.where(across == theirs, 1.0, 0.0)
        rank = jnp.sum(hits, axis=1, keepdims=True).astype(I32)
        t = across.astype(I32)
        slots.append((t & 3) * (LAYERS * CAP) + (t >> 2) * CAP + rank)
    zero = jnp.zeros((1, VIS_DEV), F32)
    values = jnp.concatenate(
        [
            w * vis[0:1, :],
            w * vis[1:2, :],
            cells[0:1, :].astype(F32),
            cells[1:2, :].astype(F32),
            zero,
            zero,
            zero,
            zero,
        ],
        0,
    )
    high = values.astype(BF16)
    rest = values - high.astype(F32)
    middle = rest.astype(BF16)
    low = (rest - middle.astype(F32)).astype(BF16)
    for group_number in range(GROUPS):
        for half in range(2):
            first = (group_number * 2 + half) * LANES
            picks = jnp.concatenate(
                [jnp.where(slots[b] == lane + first, 1.0, 0.0).astype(BF16) for b in range(blocks)], 0
            )
            total = jnp.dot(high, picks, preferred_element_type=F32)
            total += jnp.dot(middle, picks, preferred_element_type=F32)
            total += jnp.dot(low, picks, preferred_element_type=F32)
            out[group_number, half * 4 : half * 4 + 4, :] = total[0:4]
        power = jnp.sum(jnp.where(group[...] == group_number, w * w, 0.0), axis=1, keepdims=True)
        out[group_number, 8:9, :] = jnp.zeros((1, LANES), F32) + depth[0]
        out[group_number, 9:10, :] = jnp.zeros((1, LANES), F32) + power


def image_kernel(first_row, got, sky, out, vals, wtab, ltab, ntab, c16, dterm, acc, ximg, lhs_a, rhs_a, lhs_b, rhs_b):
    row0 = first_row[0]
    for half in range(2):
        for v in range(4):
            vals[v, half * LANES : (half + 1) * LANES, :] = got[:, half * 4 + v, :].T
    sub = lax.broadcasted_iota(I32, (8, LANES), 0)
    lane = lax.broadcasted_iota(I32, (8, LANES), 1)
    for sl in range(2):
        rows = (row0 + 768) + (8 + sub if sl == 0 else 7 - sub)
        l = 0.8 * rows.astype(F32) / GRID
        for sn in range(2):
            for c0 in range(BLOCKS):
                cols = 256 * c0 - 1024 + (128 + lane if sn == 0 else 127 - lane)
                m = 0.8 * cols.astype(F32) / GRID
                q = l * l + m * m
                t = (c0 * 2 + sl) * 2 + sn
                dterm[t * 8 : t * 8 + 8, :] = -q / (1.0 + jnp.sqrt(1.0 - q))
    acc[...] = jnp.zeros_like(acc)

    def tables(jc, carry):
        base = pl.multiple_of(jc * 32, 32)
        zr = vals[0, pl.ds(base, 32), :]
        zi = vals[1, pl.ds(base, 32), :]
        u = vals[2, pl.ds(base, 32), :].astype(I32)
        v = vals[3, pl.ds(base, 32), :].astype(I32)

        def put(ref, per_layer, q, x):
            for i in range(4):
                at = pl.multiple_of((jc * 4 + i) * per_layer * 8, 8) + q * 8
                ref[pl.ds(at, 8), :] = x[i * 8 : i * 8 + 8]

        w = cmul((zr, zi), sincos_phase((2 * row0 + 1551) * u - 1793 * v))
        step = sincos_phase(512 * v)
        for c0 in range(BLOCKS):
            put(wtab, 32, c0 * 2, w[0])
            put(wtab, 32, c0 * 2 + 1, w[1])
            if c0 + 1 < BLOCKS:
                w = cmul(w, step)
        half_step = sincos_phase(u)
        step = cmul(half_step, half_step)
        e = half_step
        for n in range(8):
            put(ltab, 16, n, e[0])
            put(ltab, 16, 8 + n, e[1])
            if n < 7:
                e = cmul(e, step)
        half_step = sincos_phase(v)
        step = cmul(half_step, half_step)
        e = half_step
        for n in range(16):
            put(ntab, 64, n, e[0])
            put(ntab, 64, 15 - n + 16, e[0])
            put(ntab, 64, n + 32, e[1])
            put(ntab, 64, 15 - n + 48, -e[1])
            if n < 15:
                e = cmul(e, step)
        c16[pl.ds(base, 32), :] = 2.0 * sincos_phase(32 * v)[0]
        return carry

    lax.fori_loop(0, LAYERS // 4, tables, 0)

    def expand(j, lhs, rhs):
        for s in range(8):
            ks = slice(s * LANES, (s + 1) * LANES)
            lbase = ltab[pl.ds(j * 128 + s, 16, stride=8), :]
            for q in range(32):
                row = wtab[pl.ds(j * 256 + q * 8 + s, 1), :]
                lhs[q * 16 : q * 16 + 16, ks] = (lbase * row).astype(BF16)
            c2 = c16[pl.ds(j * 8 + s, 1), :]
            for part in range(2):
                now = ntab[pl.ds(j * 512 + part * 256 + s, 16, stride=8), :]
                last = ntab[pl.ds(j * 512 + part * 256 + 128 + s, 16, stride=8), :]
                for b in range(8):
                    rhs[part * 128 + b * 16 : part * 128 + b * 16 + 16, ks] = now.astype(BF16)
                    if b < 7:
                        now, last = c2 * now - last, now

    def image(j, lhs, rhs):
        ximg[...] = lax.dot_general(
            lhs[...], rhs[...], (((1,), (1,)), ((), ())), preferred_element_type=F32
        )
        depth = got[pl.ds(j * GROUPS, 1), 8, :]
        for c0 in range(BLOCKS):
            parts = []
            for ri in range(2):
                at = (c0 * 2 + ri) * 16
                cc = ximg[at : at + 8, 0:LANES]
                cs = ximg[at : at + 8, LANES:]
                sc = ximg[at + 8 : at + 16, 0:LANES]
                ss = ximg[at + 8 : at + 16, LANES:]
                parts.append((cc - ss, cc + ss, sc + cs, sc - cs))
            (ra, rb, rp, rm), (ia, ib, ip, im) = parts
            pixels = ((ra - ip, ia + rp), (rb - im, ib + rm), (rb + im, ib - rm), (ra + ip, ia - rp))
            for k, (pr, pi) in enumerate(pixels):
                at = (c0 * 4 + k) * 8
                t = depth * dterm[at : at + 8, :]
                cos, sin = sincos_turns(t - jnp.round(t))
                acc[at : at + 8, :] += cos * pr - sin * pi

    expand(0, lhs_a, rhs_a)

    def pair(jj, carry):
        expand(2 * jj + 1, lhs_b, rhs_b)
        image(2 * jj, lhs_a, rhs_a)
        expand(jnp.minimum(2 * jj + 2, LAYERS - 1), lhs_a, rhs_a)
        image(2 * jj + 1, lhs_b, rhs_b)
        return carry

    lax.fori_loop(0, LAYERS // 2, pair, 0)

    noise = jnp.sum(got[:, 9, :], axis=0, keepdims=True)
    scale = lax.rsqrt(noise)
    back_lane = (LANES - 1) - lane
    for c0 in range(BLOCKS):
        for k in range(4):
            at = (c0 * 4 + k) * 8
            tile = acc[at : at + 8, :] * scale
            if k % 2 == 1:
                tile = jnp.take_along_axis(tile, back_lane, axis=1, mode="promise_in_bounds")
            cols = slice(c0 * 256 + (128 if k % 2 == 0 else 0), c0 * 256 + (256 if k % 2 == 0 else 128))
            if k < 2:
                out[8:16, cols] = tile - sky[8:16, cols]
            else:
                for n in range(8):
                    out[7 - n : 8 - n, cols] = tile[n : n + 1] - sky[7 - n : 8 - n, cols]


def on_device(grid_cells, visibilities, weights, layer_index, group_index, plane_depths, sky_model):
    vmem = pl.BlockSpec(memory_space=pltpu.VMEM)
    smem = pl.BlockSpec(memory_space=pltpu.SMEM)
    blocks = pl.pallas_call(
        route_kernel,
        out_shape=jax.ShapeDtypeStruct((GROUPS, MSG, LANES), F32),
        in_specs=[vmem] * 5 + [smem],
        out_specs=vmem,
        name="route",
    )(
        grid_cells,
        visibilities,
        weights.reshape(1, VIS_DEV),
        layer_index.reshape(1, VIS_DEV),
        group_index.reshape(1, VIS_DEV),
        plane_depths,
    )
    mine = lax.all_to_all(blocks, "ch", split_axis=0, concat_axis=0, tiled=True)
    got = lax.all_gather(mine, "wa", axis=0, tiled=True)
    first_row = (lax.axis_index("wa") * ROWS).astype(I32).reshape(1)
    sky = sky_model[0]
    residual = pl.pallas_call(
        image_kernel,
        out_shape=jax.ShapeDtypeStruct((ROWS, COLS), F32),
        in_specs=[smem, vmem, vmem],
        out_specs=vmem,
        scratch_shapes=[
            pltpu.VMEM((4, LAYERS * CAP, LANES), F32),
            pltpu.VMEM((LAYERS * 32 * 8, LANES), F32),
            pltpu.VMEM((LAYERS * 16 * 8, LANES), F32),
            pltpu.VMEM((LAYERS * 64 * 8, LANES), F32),
            pltpu.VMEM((LAYERS * 8, LANES), F32),
            pltpu.VMEM((64 * 8, LANES), F32),
            pltpu.VMEM((64 * 8, LANES), F32),
            pltpu.VMEM((512, 256), F32),
            pltpu.VMEM((512, 1024), BF16),
            pltpu.VMEM((256, 1024), BF16),
            pltpu.VMEM((512, 1024), BF16),
            pltpu.VMEM((256, 1024), BF16),
        ],
        compiler_params=pltpu.CompilerParams(vmem_limit_bytes=60 * 1024 * 1024),
        name="image",
    )(first_row, got, sky)
    return residual[None]


def solution(mesh):
    both = ("wa", "ch")
    return jax.shard_map(
        on_device,
        mesh=mesh,
        in_specs=(
            P(None, both),
            P(None, both),
            P(both),
            P(both),
            P(both),
            P("wa"),
            P("ch", "wa", None),
        ),
        out_specs=P("ch", "wa", None),
        check_vma=False,
    )
```

time: 396 us -> 145 us (0.37)
  waiting for transfers between devices: 178 us -> 3.95 us
  other arithmetic: 130 us -> 0 us
  blocking collectives: 32.5 us -> 107 us
  Pallas kernels: 0 us -> 30.3 us
  matrix products: 24.5 us -> 0 us
  between operations: 14.9 us -> 0.65 us
  starting transfers between devices: 11.2 us -> 3.3 us
  local copies, waits for them, and re-layouts: 4.84 us -> 0 us
    reduce_scatter x1 -> x0, waiting for transfers between devices: 167 us -> none  [on_device(): lax.psum_scatter(layer_image(row_factors, column_factors, plane_depths[0]...]
    all_gather x0 -> x1, blocking collectives: none -> 107 us  [on_device(): got = lax.all_gather(mine, 'wa', axis=0, tiled=True)]
    convert_element_type x4 -> x0, other arithmetic: 81.5 us -> none  [the longest x1 71.8 us: column_factor(): (weighted_real[:, None] * cosines - weighted_imag[:, None] * sine_values)...]
    sub x2 -> x0, other arithmetic: 35.9 us -> none  [the longest x1 35.9 us: layer_image(): return jnp.cos(screen) * real_sum - jnp.sin(screen) * imag_sum]
    psum x5 -> x0, blocking collectives: 32.5 us -> none  [over_axes(): array = lax.psum(array, axis)]
    pallas_call x0 -> x2, Pallas kernels: none -> 30.3 us  [the longest x1 28.1 us: on_device(): pl.pallas_call(image_kernel, out_shape=jax.ShapeDtypeStruct((ROWS, COLS),...]
    dot_general x1 -> x0, matrix products: 24.5 us -> none  [layer_image(): jnp.dot(row_factors, column_factors, preferred_element_type=jnp.float32)]
    neg x1 -> x0, other arithmetic: 8.44 us -> none  [row_factor(): upper_half = jnp.concatenate([real_part, -imag_part], 1)]
  transfers between devices with their start and end apart: 2 -> 1, of which waited for: 2 -> 1; matrix products, arithmetic and copies ran while one was open for 0% -> 0% of each run, Pallas kernels for 0% -> 0%
where the time goes in v1:
time: 145 us
  blocking collectives  107 us (74%)
  Pallas kernels  30.3 us (21%)
  waiting for transfers between devices  3.95 us (3%)
  starting transfers between devices  3.3 us (2%)
    all_gather x1, blocking collectives, on_device(): got = lax.all_gather(mine, 'wa', axis=0, tiled=True)  107 us
    pallas_call x1, Pallas kernels, on_device(): pl.pallas_call(image_kernel, out_shape=jax.ShapeDtypeStruct((ROWS, COLS),...  28.1 us
    all_to_all x1, waiting for transfers between devices, on_device(): mine = lax.all_to_all(blocks, 'ch', split_axis=0, concat_axis=0, tiled=True)  3.95 us
    all_to_all x1, starting transfers between devices, on_device(): mine = lax.all_to_all(blocks, 'ch', split_axis=0, concat_axis=0, tiled=True)  3.3 us
  transfers between devices with their start and end apart: 1, of which 1 were waited for; matrix products, arithmetic and copies ran while one was open for 0% of the time, Pallas kernels for 0%

profile of v1, /device:TPU:0, one launch (start us, length us, event | category | flops | bytes accessed | tf_op | source)
XLA Modules:
  0.0 144.8 jit_solution(190827676445705896)
XLA Ops:
  0.7 2.1 %route.1 = f32[4,10,128]{2,1,0:T(8,128)} custom-call(s32[2,512]{1,0:T(2,128)} %cells.1, f32[2,512]{1,0:T(2,128)} %vis.1, f32[1,512]{1,0:T(1,128)} %bitcast.7, s32[1,512]{1,0:T(1,128)} %bitcast.8, s32[1,512]{1,0:T(1,128)} %bitcast.9, f32[1]{0:T(128)S(6)} %copy.8.depth), custom_call_target="tpu_custom_call" | custom-call | tf_op jit(solution)/shard_map/route/pallas_call | solution.py:234
  2.8 3.3 %all-to-all-start = ((f32[4,10,128]{2,1,0:T(8,128)}), f32[4,10,128]{2,1,0:T(8,128)S(1)}, u32[]{:S(2)}, u32[]{:S(2)}) async-start(f32[4,10,128]{2,1,0:T(8,128)} %route.1), calls=%async_computation | async-start | bytes 65536 | tf_op jit(solution)/shard_map/all_to_all | solution.py:248
  6.1 3.9 %all-to-all-done = f32[4,10,128]{2,1,0:T(8,128)S(1)} async-done(((f32[4,10,128]{2,1,0:T(8,128)}), f32[4,10,128]{2,1,0:T(8,128)S(1)}, u32[]{:S(2)}, u32[]{:S(2)}) %all-to-all-start) | async-done | bytes 20512 | tf_op jit(solution)/shard_map/all_to_all | solution.py:248
  10.0 106.6 %all_gather.3.got = f32[128,10,128]{2,1,0:T(8,128)} all-gather(f32[4,10,128]{2,1,0:T(8,128)S(1)} %all-to-all-done), channel_id=1, replica_groups=mesh['wa'=32,'ch'=4] {'wa'}, dimensions={0}, use_global_device_ids=true | all-gather | bytes 675840 | tf_op jit(solution)/shard_map/all_gather | solution.py:249
  116.6 28.1 %image.1 = f32[16,4096]{1,0:T(8,128)} custom-call(s32[1]{0:T(128)} %bitcast.first_row, f32[128,10,128]{2,1,0:T(8,128)} %all_gather.3.got, f32[16,4096]{1,0:T(8,128)} %bitcast.6), custom_call_target="tpu_custom_call" | custom-call | tf_op jit(solution)/shard_map/image/pallas_call | solution.py:252
Async XLA Ops:
  2.8 7.2 %all-to-all-start = ((f32[4,10,128]{2,1,0:T(8,128)}), f32[4,10,128]{2,1,0:T(8,128)S(1)}, u32[]{:S(2)}, u32[]{:S(2)}) async-start(f32[4,10,128]{2,1,0:T(8,128)} %route.1), calls=%async_computation | async-start | bytes 65536 | tf_op jit(solution)/shard_map/all_to_all | solution.py:248

commit v2 on v1

--- a/solution.py
+++ b/solution.py
@@ -51,7 +51,7 @@
     return a[0] * b[0] - a[1] * b[1], a[0] * b[1] + a[1] * b[0]
 
 
-def route_kernel(cells, vis, weights, layer, group, depth, out):
+def fill_blocks(cells, vis, weights, layer, group, depth, out):
     w = weights[...]
     target_row = (layer[...] * GROUPS + group[...]).astype(F32)
     blocks = VIS_DEV // LANES
@@ -101,11 +101,50 @@
         out[group_number, 9:10, :] = jnp.zeros((1, LANES), F32) + power
 
 
-def image_kernel(first_row, got, sky, out, vals, wtab, ltab, ntab, c16, dterm, acc, ximg, lhs_a, rhs_a, lhs_b, rhs_b):
-    row0 = first_row[0]
+def exchange_kernel(mult, cells, vis, weights, layer, group, depth, vals, misc, blocks, recv, send_sem, recv_sem):
+    wa = lax.axis_index("wa")
+    ch = lax.axis_index("ch")
+    me = wa * GROUPS + ch
+    barrier = pltpu.get_barrier_semaphore()
+
+    def device(d):
+        other = lax.rem(me + lax.rem(d * mult, SOURCES), SOURCES)
+        return other // GROUPS, lax.rem(other, GROUPS)
+
+    def greet(d, carry):
+        pl.semaphore_signal(barrier, inc=1, device_id=device(d), device_id_type=pl.DeviceIdType.MESH)
+        return carry
+
+    lax.fori_loop(1, SOURCES, greet, 0)
+    fill_blocks(cells, vis, weights, layer, group, depth, blocks)
+    pl.semaphore_wait(barrier, SOURCES - 1)
+
+    def send(d, carry):
+        to = device(d)
+        pltpu.make_async_remote_copy(
+            src_ref=blocks.at[to[1]],
+            dst_ref=recv.at[me],
+            send_sem=send_sem,
+            recv_sem=recv_sem,
+            device_id=to,
+            device_id_type=pl.DeviceIdType.MESH,
+        ).start()
+        return carry
+
+    lax.fori_loop(1, SOURCES, send, 0)
+    recv[me] = blocks[ch]
+    rest = recv.at[pl.ds(0, SOURCES - 1)]
+    pltpu.make_async_copy(rest, rest, recv_sem).wait()
     for half in range(2):
         for v in range(4):
-            vals[v, half * LANES : (half + 1) * LANES, :] = got[:, half * 4 + v, :].T
+            vals[v, half * LANES : (half + 1) * LANES, :] = recv[:, half * 4 + v, :].T
+    misc[0] = recv[:, 8, :]
+    misc[1] = recv[:, 9, :]
+    pltpu.make_async_copy(rest, rest, send_sem).wait()
+
+
+def image_kernel(first_row, vals, misc, sky, out, wtab, ltab, ntab, c16, dterm, acc, ximg, lhs_a, rhs_a, lhs_b, rhs_b):
+    row0 = first_row[0]
     sub = lax.broadcasted_iota(I32, (8, LANES), 0)
     lane = lax.broadcasted_iota(I32, (8, LANES), 1)
     for sl in range(2):
@@ -182,7 +221,7 @@
         ximg[...] = lax.dot_general(
             lhs[...], rhs[...], (((1,), (1,)), ((), ())), preferred_element_type=F32
         )
-        depth = got[pl.ds(j * GROUPS, 1), 8, :]
+        depth = misc[0, pl.ds(j * GROUPS, 1), :]
         for c0 in range(BLOCKS):
             parts = []
             for ri in range(2):
@@ -211,7 +250,7 @@
 
     lax.fori_loop(0, LAYERS // 2, pair, 0)
 
-    noise = jnp.sum(got[:, 9, :], axis=0, keepdims=True)
+    noise = jnp.sum(misc[1], axis=0, keepdims=True)
     scale = lax.rsqrt(noise)
     back_lane = (LANES - 1) - lane
     for c0 in range(BLOCKS):
@@ -231,12 +270,22 @@
 def on_device(grid_cells, visibilities, weights, layer_index, group_index, plane_depths, sky_model):
     vmem = pl.BlockSpec(memory_space=pltpu.VMEM)
     smem = pl.BlockSpec(memory_space=pltpu.SMEM)
-    blocks = pl.pallas_call(
-        route_kernel,
-        out_shape=jax.ShapeDtypeStruct((GROUPS, MSG, LANES), F32),
+    vals, misc = pl.pallas_call(
+        functools.partial(exchange_kernel, 1),
+        out_shape=(
+            jax.ShapeDtypeStruct((4, LAYERS * CAP, LANES), F32),
+            jax.ShapeDtypeStruct((2, SOURCES, LANES), F32),
+        ),
         in_specs=[vmem] * 5 + [smem],
-        out_specs=vmem,
-        name="route",
+        out_specs=(vmem, vmem),
+        scratch_shapes=[
+            pltpu.VMEM((GROUPS, MSG, LANES), F32),
+            pltpu.VMEM((SOURCES, MSG, LANES), F32),
+            pltpu.SemaphoreType.DMA,
+            pltpu.SemaphoreType.DMA,
+        ],
+        compiler_params=pltpu.CompilerParams(collective_id=0, has_side_effects=True),
+        name="exchange",
     )(
         grid_cells,
         visibilities,
@@ -245,17 +294,14 @@
         group_index.reshape(1, VIS_DEV),
         plane_depths,
     )
-    mine = lax.all_to_all(blocks, "ch", split_axis=0, concat_axis=0, tiled=True)
-    got = lax.all_gather(mine, "wa", axis=0, tiled=True)
     first_row = (lax.axis_index("wa") * ROWS).astype(I32).reshape(1)
     sky = sky_model[0]
     residual = pl.pallas_call(
         image_kernel,
         out_shape=jax.ShapeDtypeStruct((ROWS, COLS), F32),
-        in_specs=[smem, vmem, vmem],
+        in_specs=[smem, vmem, vmem, vmem],
         out_specs=vmem,
         scratch_shapes=[
-            pltpu.VMEM((4, LAYERS * CAP, LANES), F32),
             pltpu.VMEM((LAYERS * 32 * 8, LANES), F32),
             pltpu.VMEM((LAYERS * 16 * 8, LANES), F32),
             pltpu.VMEM((LAYERS * 64 * 8, LANES), F32),
@@ -270,7 +316,7 @@
         ],
         compiler_params=pltpu.CompilerParams(vmem_limit_bytes=60 * 1024 * 1024),
         name="image",
-    )(first_row, got, sky)
+    )(first_row, vals, misc, sky)
     return residual[None]
 
 

time: 145 us -> 52 us (0.36)
  the two profiles are of different devices: /device:TPU:0 before, /device:TPU:1 now
where the time goes in v2:
time: 52 us; the launch traced here: 51.9 us
  Pallas kernels  51.2 us (98%)
  between operations  0.66 us (1%)
    pallas_call x1, Pallas kernels, on_device(): pl.pallas_call(image_kernel, out_shape=jax.ShapeDtypeStruct((ROWS, COLS),...  27.7 us
    pallas_call x1, Pallas kernels, on_device(): pl.pallas_call(functools.partial(exchange_kernel, 1), out_shape=(jax.Shap...  23.5 us

profile of v2, /device:TPU:1, one launch (start us, length us, event | category | flops | bytes accessed | tf_op | source)
XLA Modules:
  0.0 51.9 jit_solution(4945619061656586741)
XLA Ops:
  0.7 23.5 %exchange.1 = (f32[4,256,128]{2,1,0:T(8,128)}, f32[2,128,128]{2,1,0:T(8,128)}) custom-call(s32[2,512]{1,0:T(2,128)} %cells.1, f32[2,512]{1,0:T(2,128)} %vis.1, f32[1,512]{1,0:T(1,128)} %bitcast.7, s32[1,512]{1,0:T(1,128)} %bitcast.8, s32[1,512]{1,0:T(1,128)} %bitcast.9, f32[1]{0:T(128)S(6)} %copy.8.depth), custom_call_target="tpu_custom_call" | custom-call | tf_op jit(solution)/shard_map/exchange/pallas_call | solution.py:273
  24.1 27.7 %image.1 = f32[16,4096]{1,0:T(8,128)} custom-call(s32[1]{0:T(128)} %bitcast.first_row, f32[4,256,128]{2,1,0:T(8,128)} %get-tuple-element.7.vals, f32[2,128,128]{2,1,0:T(8,128)} %get-tuple-element.8.misc, f32[16,4096]{1,0:T(8,128)} %bitcast.6), custom_call_target="tpu_custom_call" | custom-call | tf_op jit(solution)/shard_map/image/pallas_call | solution.py:299

commit v3 on v2

--- a/solution.py
+++ b/solution.py
@@ -143,7 +143,7 @@
     pltpu.make_async_copy(rest, rest, send_sem).wait()
 
 
-def image_kernel(first_row, vals, misc, sky, out, wtab, ltab, ntab, c16, dterm, acc, ximg, lhs_a, rhs_a, lhs_b, rhs_b):
+def image_kernel(first_row, vals, misc, sky, out, wtab, ltab, ntab, c16, dterm, acc, ximg):
     row0 = first_row[0]
     sub = lax.broadcasted_iota(I32, (8, LANES), 0)
     lane = lax.broadcasted_iota(I32, (8, LANES), 1)
@@ -239,16 +239,25 @@
                 cos, sin = sincos_turns(t - jnp.round(t))
                 acc[at : at + 8, :] += cos * pr - sin * pi
 
-    expand(0, lhs_a, rhs_a)
-
-    def pair(jj, carry):
-        expand(2 * jj + 1, lhs_b, rhs_b)
-        image(2 * jj, lhs_a, rhs_a)
-        expand(jnp.minimum(2 * jj + 2, LAYERS - 1), lhs_a, rhs_a)
-        image(2 * jj + 1, lhs_b, rhs_b)
-        return carry
-
-    lax.fori_loop(0, LAYERS // 2, pair, 0)
+    def all_layers(lhs_a, rhs_a, lhs_b, rhs_b):
+        expand(0, lhs_a, rhs_a)
+
+        def pair(jj, carry):
+            expand(2 * jj + 1, lhs_b, rhs_b)
+            image(2 * jj, lhs_a, rhs_a)
+            expand(jnp.minimum(2 * jj + 2, LAYERS - 1), lhs_a, rhs_a)
+            image(2 * jj + 1, lhs_b, rhs_b)
+            return carry
+
+        lax.fori_loop(0, LAYERS // 2, pair, 0)
+
+    pl.run_scoped(
+        all_layers,
+        pltpu.VMEM((512, 1024), BF16),
+        pltpu.VMEM((256, 1024), BF16),
+        pltpu.VMEM((512, 1024), BF16),
+        pltpu.VMEM((256, 1024), BF16),
+    )
 
     noise = jnp.sum(misc[1], axis=0, keepdims=True)
     scale = lax.rsqrt(noise)
@@ -309,10 +318,6 @@
             pltpu.VMEM((64 * 8, LANES), F32),
             pltpu.VMEM((64 * 8, LANES), F32),
             pltpu.VMEM((512, 256), F32),
-            pltpu.VMEM((512, 1024), BF16),
-            pltpu.VMEM((256, 1024), BF16),
-            pltpu.VMEM((512, 1024), BF16),
-            pltpu.VMEM((256, 1024), BF16),
         ],
         compiler_params=pltpu.CompilerParams(vmem_limit_bytes=60 * 1024 * 1024),
         name="image",

time: 52 us -> 46.3 us (0.89)
  Pallas kernels: 51.2 us -> 45.5 us
    pallas_call x1, Pallas kernels: 27.7 us -> 22 us  [on_device(): pl.pallas_call(image_kernel, out_shape=jax.ShapeDtypeStruct((ROWS, COLS),...]
where the time goes in v3:
time: 46.3 us; the launch traced here: 46.2 us
  Pallas kernels  45.5 us (98%)
  between operations  0.66 us (1%)
    pallas_call x1, Pallas kernels, on_device(): pl.pallas_call(functools.partial(exchange_kernel, 1), out_shape=(jax.Shap...  23.5 us
    pallas_call x1, Pallas kernels, on_device(): pl.pallas_call(image_kernel, out_shape=jax.ShapeDtypeStruct((ROWS, COLS),...  22 us

profile of v3, /device:TPU:1, one launch (start us, length us, event | category | flops | bytes accessed | tf_op | source)
XLA Modules:
  0.0 46.2 jit_solution(1504986326732866947)
XLA Ops:
  0.7 23.5 %exchange.1 = (f32[4,256,128]{2,1,0:T(8,128)}, f32[2,128,128]{2,1,0:T(8,128)}) custom-call(s32[2,512]{1,0:T(2,128)} %cells.1, f32[2,512]{1,0:T(2,128)} %vis.1, f32[1,512]{1,0:T(1,128)} %bitcast.7, s32[1,512]{1,0:T(1,128)} %bitcast.8, s32[1,512]{1,0:T(1,128)} %bitcast.9, f32[1]{0:T(128)S(6)} %copy.8.depth), custom_call_target="tpu_custom_call" | custom-call | tf_op jit(solution)/shard_map/exchange/pallas_call | solution.py:282
  24.1 22.0 %image.1 = f32[16,4096]{1,0:T(8,128)} custom-call(s32[1]{0:T(128)} %bitcast.first_row, f32[4,256,128]{2,1,0:T(8,128)} %get-tuple-element.7.vals, f32[2,128,128]{2,1,0:T(8,128)} %get-tuple-element.8.misc, f32[16,4096]{1,0:T(8,128)} %bitcast.6), custom_call_target="tpu_custom_call" | custom-call | tf_op jit(solution)/shard_map/image/pallas_call | solution.py:308

commit v4 on v1

v4 whole, which is shorter than its diff:
```python
import functools
import math

import jax
import jax.numpy as jnp
from jax import lax
from jax.experimental import pallas as pl
from jax.experimental.pallas import tpu as pltpu
from jax.sharding import PartitionSpec as P

F32 = jnp.float32
BF16 = jnp.bfloat16
I32 = jnp.int32

GRID = 8192
LAYERS = 32
GROUPS = 4
SOURCES = 128
CAP = 8
LANES = 128
VIS_DEV = 512
ROWS = 16
COLS = 4096
BLOCKS = COLS // 256
ALL = SOURCES - 1

SIN_C = (4.442882919124344, -7.308245686509099, 3.6063542184331383, -0.8461116503741475, 0.10982451642439378)
COS_C = (1.4142134962552289, -6.978850948563853, 5.7394603769076955, -1.8835579059892091, 0.31068802753070307)


def horner(g, coefs):
    total = coefs[-1] * g + coefs[-2]
    for c in coefs[-3::-1]:
        total = total * g + c
    return total


def sincos_turns(f):
    g = f * f
    s = horner(g, SIN_C) * f
    c = horner(g, COS_C)
    return 1.0 - s * s, s * c


def half_turns(f):
    g = f * f
    return horner(g, SIN_C) * f, horner(g, COS_C)


def csquare(a):
    return a[0] * a[0] - a[1] * a[1], 2.0 * (a[0] * a[1])


def sincos_phase(p):
    q = ((p + GRID) & (2 * GRID - 1)) - GRID
    return sincos_turns(q.astype(F32) * (1.0 / (2 * GRID)))


def cmul(a, b):
    return a[0] * b[0] - a[1] * b[1], a[0] * b[1] + a[1] * b[0]


def fill_blocks(cells, vis, weights, layer, group, depth, blocks, notes):
    w = weights[...]
    target_row = (layer[...] * GROUPS + group[...]).astype(F32)
    pieces = VIS_DEV // LANES
    lane = lax.broadcasted_iota(I32, (LANES, LANES), 1)
    sub = lax.broadcasted_iota(I32, (LANES, LANES), 0)
    slots = []
    for b in range(pieces):
        mine = target_row[:, b * LANES : (b + 1) * LANES]
        across = jnp.broadcast_to(mine, (LANES, LANES)).T
        hits = jnp.where((across == mine) & (lane < sub), 1.0, 0.0)
        for other in range(b):
            theirs = target_row[:, other * LANES : (other + 1) * LANES]
            hits += jnp.where(across == theirs, 1.0, 0.0)
        rank = jnp.sum(hits, axis=1, keepdims=True).astype(I32)
        t = across.astype(I32)
        slots.append((t & 3) * (LAYERS * CAP) + (t >> 2) * CAP + rank)
    zero = jnp.zeros((1, VIS_DEV), F32)
    values = jnp.concatenate(
        [
            w * vis[0:1, :],
            w * vis[1:2, :],
            cells[0:1, :].astype(F32),
            cells[1:2, :].astype(F32),
            zero,
            zero,
            zero,
            zero,
        ],
        0,
    )
    high = values.astype(BF16)
    rest = values - high.astype(F32)
    middle = rest.astype(BF16)
    low = (rest - middle.astype(F32)).astype(BF16)
    for group_number in range(GROUPS):
        for half in range(2):
            first = (group_number * 2 + half) * LANES
            picks = jnp.concatenate(
                [jnp.where(slots[b] == lane + first, 1.0, 0.0).astype(BF16) for b in range(pieces)], 0
            )
            total = jnp.dot(high, picks, preferred_element_type=F32)
            total += jnp.dot(middle, picks, preferred_element_type=F32)
            total += jnp.dot(low, picks, preferred_element_type=F32)
            blocks[group_number, half] = total[0:4]
        power = jnp.sum(jnp.where(group[...] == group_number, w * w, 0.0), axis=1, keepdims=True)
        notes[group_number, 0:1, :] = jnp.zeros((1, LANES), F32) + depth[0]
        notes[group_number, 1:2, :] = jnp.zeros((1, LANES), F32) + power


def kernel(
    cells, vis, weights, layer, group, depth, sky, out,
    blocks, notes, recv, heard, vals, wtab, ltab, ntab, c8, dterm, stab, ctab, acc, x_a, x_b,
    send_sem, recv_sem, note_send, note_recv,
):
    wa = lax.axis_index("wa")
    ch = lax.axis_index("ch")
    me = wa * GROUPS + ch
    row0 = wa * ROWS
    barrier = pltpu.get_barrier_semaphore()
    mesh_id = pl.DeviceIdType.MESH

    def each_peer(act):
        for i in range(1, GROUPS):
            act(wa, lax.rem(ch + i, GROUPS))

        def several(d, carry):
            other = lax.rem(wa + d, LAYERS)
            for c in range(GROUPS):
                act(other, c)
            return carry

        lax.fori_loop(1, LAYERS, several, 0)

    def greet(w, c):
        pl.semaphore_signal(barrier, inc=1, device_id=(w, c), device_id_type=mesh_id)

    each_peer(greet)
    fill_blocks(cells, vis, weights, layer, group, depth, blocks, notes)
    sub = lax.broadcasted_iota(I32, (8, LANES), 0)
    lane = lax.broadcasted_iota(I32, (8, LANES), 1)
    for sl in range(2):
        rows = (row0 + 768) + (8 + sub if sl == 0 else 7 - sub)
        l = 0.8 * rows.astype(F32) / GRID
        for sn in range(2):
            for c0 in range(BLOCKS):
                cols = 256 * c0 - 1024 + (128 + lane if sn == 0 else 127 - lane)
                m = 0.8 * cols.astype(F32) / GRID
                q = l * l + m * m
                t = (c0 * 2 + sl) * 2 + sn
                dterm[t * 8 : t * 8 + 8, :] = -q / (1.0 + jnp.sqrt(1.0 - q))
    acc[...] = jnp.zeros_like(acc)
    pl.semaphore_wait(barrier, ALL)

    def send_note(w, c):
        pltpu.make_async_remote_copy(
            src_ref=notes.at[c], dst_ref=heard.at[me], send_sem=note_send, recv_sem=note_recv,
            device_id=(w, c), device_id_type=mesh_id,
        ).start()

    each_peer(send_note)
    for half in range(2):

        def send(w, c):
            pltpu.make_async_remote_copy(
                src_ref=blocks.at[c, half], dst_ref=recv.at[half, me],
                send_sem=send_sem.at[half], recv_sem=recv_sem.at[half],
                device_id=(w, c), device_id_type=mesh_id,
            ).start()

        each_peer(send)
    for half in range(2):
        recv[half, me] = blocks[ch, half]
    heard[me] = notes[ch]

    all_notes = heard.at[pl.ds(0, ALL)]
    pltpu.make_async_copy(all_notes, all_notes, note_recv).wait()

    def screens(j, carry):
        w = heard[j * GROUPS, 0:1, :]
        for p in range(64):
            t = w * dterm[p * 8 : p * 8 + 8, :]
            s, c = half_turns(t - jnp.round(t))
            stab[j, p * 8 : p * 8 + 8, :] = s
            ctab[j, p * 8 : p * 8 + 8, :] = c
        return carry

    lax.fori_loop(0, LAYERS, screens, 0)

    def tables(jc, carry):
        base = pl.multiple_of(jc * 32, 32)
        zr = vals[0, pl.ds(base, 32), :]
        zi = vals[1, pl.ds(base, 32), :]
        u = vals[2, pl.ds(base, 32), :].astype(I32)
        v = vals[3, pl.ds(base, 32), :].astype(I32)

        def put(ref, per_layer, q, x):
            for i in range(4):
                at = pl.multiple_of((jc * 4 + i) * per_layer * 8, 8) + q * 8
                ref[pl.ds(at, 8), :] = x[i * 8 : i * 8 + 8]

        w = cmul((zr, zi), sincos_phase((2 * row0 + 1551) * u - 1793 * v))
        step = sincos_phase(512 * v)
        for c0 in range(BLOCKS):
            put(wtab, 32, c0 * 2, w[0])
            put(wtab, 32, c0 * 2 + 1, w[1])
            if c0 + 1 < BLOCKS:
                w = cmul(w, step)
        e = sincos_phase(u)
        step = csquare(e)
        for n in range(8):
            put(ltab, 16, n, e[0])
            put(ltab, 16, 8 + n, e[1])
            if n < 7:
                e = cmul(e, step)
        e = sincos_phase(v)
        step = csquare(e)
        eighth = csquare(csquare(csquare(step)))
        for n in range(8):
            put(ntab, 32, n, e[0])
            put(ntab, 32, 15 - n, e[0])
            put(ntab, 32, 16 + n, e[1])
            put(ntab, 32, 31 - n, e[1])
            if n < 7:
                e = cmul(e, step)
        c8[pl.ds(base, 32), :] = 2.0 * eighth[0]
        return carry

    def expand(j, lhs, rhs):
        for s in range(8):
            ks = slice(s * LANES, (s + 1) * LANES)
            lbase = ltab[pl.ds(j * 128 + s, 16, stride=8), :]
            for q in range(32):
                row = wtab[pl.ds(j * 256 + q * 8 + s, 1), :]
                lhs[q * 16 : q * 16 + 16, ks] = (lbase * row).astype(BF16)
            c2 = c8[pl.ds(j * 8 + s, 1), :]
            for part in range(2):
                low = ntab[pl.ds(j * 256 + part * 128 + s, 8, stride=8), :]
                back = ntab[pl.ds(j * 256 + part * 128 + 64 + s, 8, stride=8), :]
                high = c2 * low - back if part == 0 else c2 * low + back
                for b in range(8):
                    at = part * 128 + b * 16
                    rhs[at : at + 16, ks] = jnp.concatenate([low, high], 0).astype(BF16)
                    if b < 7:
                        low = c2 * high - low
                        high = c2 * low - high

    def multiply(ximg, lhs, rhs):
        ximg[...] = lax.dot_general(
            lhs[...], rhs[...], (((1,), (1,)), ((), ())), preferred_element_type=F32
        )

    def image(j, ximg):
        for c0 in range(BLOCKS):
            parts = []
            for ri in range(2):
                at = (c0 * 2 + ri) * 16
                cc = ximg[at : at + 8, 0:LANES]
                cs = ximg[at : at + 8, LANES:]
                sc = ximg[at + 8 : at + 16, 0:LANES]
                ss = ximg[at + 8 : at + 16, LANES:]
                parts.append((cc - ss, cc + ss, sc + cs, sc - cs))
            (ra, rb, rp, rm), (ia, ib, ip, im) = parts
            pixels = ((ra - ip, ia + rp), (rb - im, ib + rm), (rb + im, ib - rm), (ra + ip, ia - rp))
            for k, (pr, pi) in enumerate(pixels):
                at = (c0 * 4 + k) * 8
                s = stab[j, at : at + 8, :]
                c = ctab[j, at : at + 8, :]
                acc[at : at + 8, :] += pr - s * (s * pr + c * pi)

    def all_layers(lhs_a, rhs_a, lhs_b, rhs_b):
        def part(half, carry):
            arriving = recv.at[half, pl.ds(0, ALL)]
            pltpu.make_async_copy(arriving, arriving, recv_sem.at[half]).wait()
            for v in range(4):
                vals[v, pl.ds(pl.multiple_of(half * LANES, LANES), LANES), :] = recv[half, :, v, :].T
            first = half * (LAYERS // 2)
            lax.fori_loop(half * 4, half * 4 + 4, tables, 0)
            expand(first, lhs_a, rhs_a)
            multiply(x_a, lhs_a, rhs_a)
            expand(first + 1, lhs_b, rhs_b)

            def pair(jj, carry):
                j = first + 2 * jj
                last = first + LAYERS // 2 - 1
                multiply(x_b, lhs_b, rhs_b)
                image(j, x_a)
                expand(jnp.minimum(j + 2, last), lhs_a, rhs_a)
                multiply(x_a, lhs_a, rhs_a)
                image(j + 1, x_b)
                expand(jnp.minimum(j + 3, last), lhs_b, rhs_b)
                return carry

            lax.fori_loop(0, LAYERS // 4, pair, 0)
            return carry

        lax.fori_loop(0, 2, part, 0)

    pl.run_scoped(
        all_layers,
        pltpu.VMEM((512, 1024), BF16),
        pltpu.VMEM((256, 1024), BF16),
        pltpu.VMEM((512, 1024), BF16),
        pltpu.VMEM((256, 1024), BF16),
    )

    noise = jnp.sum(heard[:, 1, :], axis=0, keepdims=True)
    scale = lax.rsqrt(noise)
    back_lane = (LANES - 1) - lane
    for c0 in range(BLOCKS):
        for k in range(4):
            at = (c0 * 4 + k) * 8
            tile = acc[at : at + 8, :] * scale
            if k % 2 == 1:
                tile = jnp.take_along_axis(tile, back_lane, axis=1, mode="promise_in_bounds")
            cols = slice(c0 * 256 + (128 if k % 2 == 0 else 0), c0 * 256 + (256 if k % 2 == 0 else 128))
            if k < 2:
                out[8:16, cols] = tile - sky[8:16, cols]
            else:
                for n in range(8):
                    out[7 - n : 8 - n, cols] = tile[n : n + 1] - sky[7 - n : 8 - n, cols]
    pltpu.make_async_copy(all_notes, all_notes, note_send).wait()
    for half in range(2):
        sent = recv.at[half, pl.ds(0, ALL)]
        pltpu.make_async_copy(sent, sent, send_sem.at[half]).wait()


def on_device(grid_cells, visibilities, weights, layer_index, group_index, plane_depths, sky_model):
    vmem = pl.BlockSpec(memory_space=pltpu.VMEM)
    smem = pl.BlockSpec(memory_space=pltpu.SMEM)
    residual = pl.pallas_call(
        kernel,
        out_shape=jax.ShapeDtypeStruct((ROWS, COLS), F32),
        in_specs=[vmem] * 5 + [smem, vmem],
        out_specs=vmem,
        scratch_shapes=[
            pltpu.VMEM((GROUPS, 2, 4, LANES), F32),
            pltpu.VMEM((GROUPS, 2, LANES), F32),
            pltpu.VMEM((2, SOURCES, 4, LANES), F32),
            pltpu.VMEM((SOURCES, 2, LANES), F32),
            pltpu.VMEM((4, LAYERS * CAP, LANES), F32),
            pltpu.VMEM((LAYERS * 32 * 8, LANES), F32),
            pltpu.VMEM((LAYERS * 16 * 8, LANES), F32),
            pltpu.VMEM((LAYERS * 32 * 8, LANES), F32),
            pltpu.VMEM((LAYERS * 8, LANES), F32),
            pltpu.VMEM((64 * 8, LANES), F32),
            pltpu.VMEM((LAYERS, 64 * 8, LANES), F32),
            pltpu.VMEM((LAYERS, 64 * 8, LANES), F32),
            pltpu.VMEM((64 * 8, LANES), F32),
            pltpu.VMEM((512, 256), F32),
            pltpu.VMEM((512, 256), F32),
            pltpu.SemaphoreType.DMA((2,)),
            pltpu.SemaphoreType.DMA((2,)),
            pltpu.SemaphoreType.DMA,
            pltpu.SemaphoreType.DMA,
        ],
        compiler_params=pltpu.CompilerParams(
            collective_id=0, has_side_effects=True, vmem_limit_bytes=60 * 1024 * 1024
        ),
        name="cycle",
    )(
        grid_cells,
        visibilities,
        weights.reshape(1, VIS_DEV),
        layer_index.reshape(1, VIS_DEV),
        group_index.reshape(1, VIS_DEV),
        plane_depths,
        sky_model[0],
    )
    return residual[None]


def solution(mesh):
    both = ("wa", "ch")
    return jax.shard_map(
        on_device,
        mesh=mesh,
        in_specs=(
            P(None, both),
            P(None, both),
            P(both),
            P(both),
            P(both),
            P("wa"),
            P("ch", "wa", None),
        ),
        out_specs=P("ch", "wa", None),
        check_vma=False,
    )
```

time: 145 us -> 42.9 us (0.30)
  the two profiles are of different devices: /device:TPU:0 before, /device:TPU:1 now
where the time goes in v4:
time: 42.9 us; the launch traced here: 42.7 us
  Pallas kernels  40.4 us (94%)
  local copies, waits for them, and re-layouts  1.67 us (4%)
  between operations  0.66 us (2%)
    pallas_call x1, Pallas kernels, on_device(): pl.pallas_call(kernel, out_shape=jax.ShapeDtypeStruct((ROWS, COLS), F32),...  40.4 us
    unnamed x1, local copies, waits for them, and re-layouts  1.67 us

profile of v4, /device:TPU:1, one launch (start us, length us, event | category | flops | bytes accessed | tf_op | source)
XLA Modules:
  0.0 42.7 jit_solution(16654253754216177950)
XLA Ops:
  0.7 40.4 %cycle.1 = f32[16,4096]{1,0:T(8,128)} custom-call(s32[2,512]{1,0:T(2,128)} %cells.1, f32[2,512]{1,0:T(2,128)} %vis.1, f32[1,512]{1,0:T(1,128)} %bitcast.7, s32[1,512]{1,0:T(1,128)} %bitcast.8, s32[1,512]{1,0:T(1,128)} %bitcast.9, f32[1]{0:T(128)S(6)} %copy.9.depth, f32[16,4096]{1,0:T(8,128)} %bitcast.6), custom_call_target="tpu_custom_call" | custom-call | tf_op jit(solution)/shard_map/cycle/pallas_call | solution.py:333
  41.0 1.7 %copy.10 = f32[1,16,4096]{2,1,0:T(8,128)} copy(f32[1,16,4096]{2,1,0:T(8,128)} %bitcast.5) | data formatting | bytes 524288

commit v5 on v4

--- a/solution.py
+++ b/solution.py
@@ -23,6 +23,7 @@
 COLS = 4096
 BLOCKS = COLS // 256
 ALL = SOURCES - 1
+STAGES = ((0, 0), (0, 1), (1, 0), (3, 0), (1, 1), (3, 1), (2, 0), (2, 1))
 
 SIN_C = (4.442882919124344, -7.308245686509099, 3.6063542184331383, -0.8461116503741475, 0.10982451642439378)
 COS_C = (1.4142134962552289, -6.978850948563853, 5.7394603769076955, -1.8835579059892091, 0.31068802753070307)
@@ -60,7 +61,7 @@
     return a[0] * b[0] - a[1] * b[1], a[0] * b[1] + a[1] * b[0]
 
 
-def fill_blocks(cells, vis, weights, layer, group, depth, blocks, notes):
+def fill_blocks(cells, vis, weights, layer, group, blocks, notes):
     w = weights[...]
     target_row = (layer[...] * GROUPS + group[...]).astype(F32)
     pieces = VIS_DEV // LANES
@@ -106,14 +107,13 @@
             total += jnp.dot(low, picks, preferred_element_type=F32)
             blocks[group_number, half] = total[0:4]
         power = jnp.sum(jnp.where(group[...] == group_number, w * w, 0.0), axis=1, keepdims=True)
-        notes[group_number, 0:1, :] = jnp.zeros((1, LANES), F32) + depth[0]
-        notes[group_number, 1:2, :] = jnp.zeros((1, LANES), F32) + power
+        notes[group_number] = jnp.zeros((1, LANES), F32) + power
 
 
 def kernel(
     cells, vis, weights, layer, group, depth, sky, out,
-    blocks, notes, recv, heard, vals, wtab, ltab, ntab, c8, dterm, stab, ctab, acc, x_a, x_b,
-    send_sem, recv_sem, note_send, note_recv,
+    blocks, notes, recv, heard, mydepth, depths, vals, wtab, ltab, ntab, c8, dterm, stab, ctab, acc, x_a, x_b,
+    send_sem, recv_sem, note_send, note_recv, depth_send, depth_recv,
 ):
     wa = lax.axis_index("wa")
     ch = lax.axis_index("ch")
@@ -138,7 +138,8 @@
         pl.semaphore_signal(barrier, inc=1, device_id=(w, c), device_id_type=mesh_id)
 
     each_peer(greet)
-    fill_blocks(cells, vis, weights, layer, group, depth, blocks, notes)
+    mydepth[0] = jnp.zeros((1, LANES), F32) + depth[0]
+    fill_blocks(cells, vis, weights, layer, group, blocks, notes)
     sub = lax.broadcasted_iota(I32, (8, LANES), 0)
     lane = lax.broadcasted_iota(I32, (8, LANES), 1)
     for sl in range(2):
@@ -154,13 +155,17 @@
     acc[...] = jnp.zeros_like(acc)
     pl.semaphore_wait(barrier, ALL)
 
-    def send_note(w, c):
-        pltpu.make_async_remote_copy(
-            src_ref=notes.at[c], dst_ref=heard.at[me], send_sem=note_send, recv_sem=note_recv,
-            device_id=(w, c), device_id_type=mesh_id,
-        ).start()
-
-    each_peer(send_note)
+    x, zy = wa // 8, lax.rem(wa, 8)
+    z, y = zy // 4, lax.rem(zy, 4)
+    for i, (dx, dz) in enumerate(STAGES):
+        for dy in range(4):
+            if dx or dz or dy:
+                to = lax.rem(x + dx, 4) * 8 + lax.rem(z + dz, 2) * 4 + lax.rem(y + dy, 4)
+                pltpu.make_async_remote_copy(
+                    src_ref=mydepth.at[0], dst_ref=depths.at[wa],
+                    send_sem=depth_send, recv_sem=depth_recv.at[i],
+                    device_id=(to, lax.rem(ch + 2 * dz, GROUPS)), device_id_type=mesh_id,
+                ).start()
     for half in range(2):
 
         def send(w, c):
@@ -171,23 +176,35 @@
             ).start()
 
         each_peer(send)
+
+    def send_note(w, c):
+        pltpu.make_async_remote_copy(
+            src_ref=notes.at[c], dst_ref=heard.at[me], send_sem=note_send, recv_sem=note_recv,
+            device_id=(w, c), device_id_type=mesh_id,
+        ).start()
+
+    each_peer(send_note)
     for half in range(2):
         recv[half, me] = blocks[ch, half]
     heard[me] = notes[ch]
-
-    all_notes = heard.at[pl.ds(0, ALL)]
-    pltpu.make_async_copy(all_notes, all_notes, note_recv).wait()
-
-    def screens(j, carry):
-        w = heard[j * GROUPS, 0:1, :]
-        for p in range(64):
-            t = w * dterm[p * 8 : p * 8 + 8, :]
-            s, c = half_turns(t - jnp.round(t))
-            stab[j, p * 8 : p * 8 + 8, :] = s
-            ctab[j, p * 8 : p * 8 + 8, :] = c
-        return carry
-
-    lax.fori_loop(0, LAYERS, screens, 0)
+    depths[wa] = mydepth[0]
+
+    for i, (dx, dz) in enumerate(STAGES):
+        some = depths.at[pl.ds(0, 4 if i else 3)]
+        pltpu.make_async_copy(some, some, depth_recv.at[i]).wait()
+        first = lax.rem(x + (4 - dx), 4) * 8 + lax.rem(z + dz, 2) * 4
+
+        def screens(n, carry):
+            j = first + n
+            w = depths[j]
+            for p in range(64):
+                t = w * dterm[p * 8 : p * 8 + 8, :]
+                s, c = half_turns(t - jnp.round(t))
+                stab[j, p * 8 : p * 8 + 8, :] = s
+                ctab[j, p * 8 : p * 8 + 8, :] = c
+            return carry
+
+        lax.fori_loop(0, 4, screens, 0)
 
     def tables(jc, carry):
         base = pl.multiple_of(jc * 32, 32)
@@ -270,33 +287,34 @@
                 c = ctab[j, at : at + 8, :]
                 acc[at : at + 8, :] += pr - s * (s * pr + c * pi)
 
+    def arrive(half):
+        arriving = recv.at[half, pl.ds(0, ALL)]
+        pltpu.make_async_copy(arriving, arriving, recv_sem.at[half]).wait()
+        for v in range(4):
+            vals[v, half * LANES : (half + 1) * LANES, :] = recv[half, :, v, :].T
+
     def all_layers(lhs_a, rhs_a, lhs_b, rhs_b):
-        def part(half, carry):
-            arriving = recv.at[half, pl.ds(0, ALL)]
-            pltpu.make_async_copy(arriving, arriving, recv_sem.at[half]).wait()
-            for v in range(4):
-                vals[v, pl.ds(pl.multiple_of(half * LANES, LANES), LANES), :] = recv[half, :, v, :].T
-            first = half * (LAYERS // 2)
-            lax.fori_loop(half * 4, half * 4 + 4, tables, 0)
-            expand(first, lhs_a, rhs_a)
-            multiply(x_a, lhs_a, rhs_a)
-            expand(first + 1, lhs_b, rhs_b)
-
-            def pair(jj, carry):
-                j = first + 2 * jj
-                last = first + LAYERS // 2 - 1
+        arrive(0)
+        tables(0, 0)
+        expand(0, lhs_a, rhs_a)
+        multiply(x_a, lhs_a, rhs_a)
+        expand(1, lhs_b, rhs_b)
+
+        def several(jj, carry):
+            tables(jnp.minimum(jj + 1, LAYERS // 4 - 1), 0)
+            for i in range(0, 4, 2):
+                j = 4 * jj + i
                 multiply(x_b, lhs_b, rhs_b)
                 image(j, x_a)
-                expand(jnp.minimum(j + 2, last), lhs_a, rhs_a)
+                expand(jnp.minimum(j + 2, LAYERS - 1), lhs_a, rhs_a)
                 multiply(x_a, lhs_a, rhs_a)
                 image(j + 1, x_b)
-                expand(jnp.minimum(j + 3, last), lhs_b, rhs_b)
-                return carry
-
-            lax.fori_loop(0, LAYERS // 4, pair, 0)
+                expand(jnp.minimum(j + 3, LAYERS - 1), lhs_b, rhs_b)
             return carry
 
-        lax.fori_loop(0, 2, part, 0)
+        lax.fori_loop(0, LAYERS // 8 - 1, several, 0)
+        arrive(1)
+        lax.fori_loop(LAYERS // 8 - 1, LAYERS // 4, several, 0)
 
     pl.run_scoped(
         all_layers,
@@ -306,7 +324,9 @@
         pltpu.VMEM((256, 1024), BF16),
     )
 
-    noise = jnp.sum(heard[:, 1, :], axis=0, keepdims=True)
+    all_notes = heard.at[pl.ds(0, ALL)]
+    pltpu.make_async_copy(all_notes, all_notes, note_recv).wait()
+    noise = jnp.sum(heard[...], axis=0)
     scale = lax.rsqrt(noise)
     back_lane = (LANES - 1) - lane
     for c0 in range(BLOCKS):
@@ -322,6 +342,8 @@
                 for n in range(8):
                     out[7 - n : 8 - n, cols] = tile[n : n + 1] - sky[7 - n : 8 - n, cols]
     pltpu.make_async_copy(all_notes, all_notes, note_send).wait()
+    others = depths.at[pl.ds(0, LAYERS - 1)]
+    pltpu.make_async_copy(others, others, depth_send).wait()
     for half in range(2):
         sent = recv.at[half, pl.ds(0, ALL)]
         pltpu.make_async_copy(sent, sent, send_sem.at[half]).wait()
@@ -337,9 +359,11 @@
         out_specs=vmem,
         scratch_shapes=[
             pltpu.VMEM((GROUPS, 2, 4, LANES), F32),
-            pltpu.VMEM((GROUPS, 2, LANES), F32),
+            pltpu.VMEM((GROUPS, 1, LANES), F32),
             pltpu.VMEM((2, SOURCES, 4, LANES), F32),
-            pltpu.VMEM((SOURCES, 2, LANES), F32),
+            pltpu.VMEM((SOURCES, 1, LANES), F32),
+            pltpu.VMEM((1, 1, LANES), F32),
+            pltpu.VMEM((LAYERS, 1, LANES), F32),
             pltpu.VMEM((4, LAYERS * CAP, LANES), F32),
             pltpu.VMEM((LAYERS * 32 * 8, LANES), F32),
             pltpu.VMEM((LAYERS * 16 * 8, LANES), F32),
@@ -355,6 +379,8 @@
             pltpu.SemaphoreType.DMA((2,)),
             pltpu.SemaphoreType.DMA,
             pltpu.SemaphoreType.DMA,
+            pltpu.SemaphoreType.DMA,
+            pltpu.SemaphoreType.DMA((len(STAGES),)),
         ],
         compiler_params=pltpu.CompilerParams(
             collective_id=0, has_side_effects=True, vmem_limit_bytes=60 * 1024 * 1024

time: 42.9 us -> 39.4 us (0.918)
  Pallas kernels: 40.4 us -> 36.9 us
    pallas_call x1, Pallas kernels: 40.4 us -> 36.9 us  [on_device(): pl.pallas_call(kernel, out_shape=jax.ShapeDtypeStruct((ROWS, COLS), F32),...]
where the time goes in v5:
time: 39.4 us; the launch traced here: 39.2 us
  Pallas kernels  36.9 us (94%)
  local copies, waits for them, and re-layouts  1.67 us (4%)
  between operations  0.66 us (2%)
    pallas_call x1, Pallas kernels, on_device(): pl.pallas_call(kernel, out_shape=jax.ShapeDtypeStruct((ROWS, COLS), F32),...  36.9 us
    unnamed x1, local copies, waits for them, and re-layouts  1.67 us

profile of v5, /device:TPU:1, one launch (start us, length us, event | category | flops | bytes accessed | tf_op | source)
XLA Modules:
  0.0 39.2 jit_solution(2850524460421326369)
XLA Ops:
  0.7 36.9 %cycle.1 = f32[16,4096]{1,0:T(8,128)} custom-call(s32[2,512]{1,0:T(2,128)} %cells.1, f32[2,512]{1,0:T(2,128)} %vis.1, f32[1,512]{1,0:T(1,128)} %bitcast.7, s32[1,512]{1,0:T(1,128)} %bitcast.8, s32[1,512]{1,0:T(1,128)} %bitcast.9, f32[1]{0:T(128)S(6)} %copy.9.depth, f32[16,4096]{1,0:T(8,128)} %bitcast.6), custom_call_target="tpu_custom_call" | custom-call | tf_op jit(solution)/shard_map/cycle/pallas_call | solution.py:355
  37.5 1.7 %copy.10 = f32[1,16,4096]{2,1,0:T(8,128)} copy(f32[1,16,4096]{2,1,0:T(8,128)} %bitcast.5) | data formatting | bytes 524288

commit v6 on v5

--- a/solution.py
+++ b/solution.py
@@ -23,6 +23,7 @@
 COLS = 4096
 BLOCKS = COLS // 256
 ALL = SOURCES - 1
+FAR_FIRST = (2, 1, 3, 0)
 STAGES = ((0, 0), (0, 1), (1, 0), (3, 0), (1, 1), (3, 1), (2, 0), (2, 1))
 
 SIN_C = (4.442882919124344, -7.308245686509099, 3.6063542184331383, -0.8461116503741475, 0.10982451642439378)
@@ -111,7 +112,8 @@
 
 
 def kernel(
-    cells, vis, weights, layer, group, depth, sky, out,
+    cells_hbm, vis_hbm, weights_hbm, layer_hbm, group_hbm, depth_hbm, out,
+    cells, vis, weights, layer, group, depth, load_sem,
     blocks, notes, recv, heard, mydepth, depths, vals, wtab, ltab, ntab, c8, dterm, stab, ctab, acc, x_a, x_b,
     send_sem, recv_sem, note_send, note_recv, depth_send, depth_recv,
 ):
@@ -119,25 +121,47 @@
     ch = lax.axis_index("ch")
     me = wa * GROUPS + ch
     row0 = wa * ROWS
+    loads = [
+        pltpu.make_async_copy(src, dst, load_sem.at[i])
+        for i, (src, dst) in enumerate(
+            (
+                (cells_hbm, cells),
+                (vis_hbm, vis),
+                (weights_hbm, weights),
+                (layer_hbm, layer),
+                (group_hbm, group),
+                (depth_hbm, depth),
+            )
+        )
+    ]
+    for load in loads:
+        load.start()
     barrier = pltpu.get_barrier_semaphore()
     mesh_id = pl.DeviceIdType.MESH
 
+    x, zy = wa // 8, lax.rem(wa, 8)
+    z, y = zy // 4, lax.rem(zy, 4)
+
+    def moved(dx, dz, dy):
+        return lax.rem(x + dx, 4) * 8 + lax.rem(z + dz, 2) * 4 + lax.rem(y + dy, 4)
+
     def each_peer(act):
+        for dx in FAR_FIRST:
+            for dz in (1, 0):
+                for dy in FAR_FIRST:
+                    if dx or dz or dy:
+                        to = moved(dx, dz, dy)
+                        for c in range(GROUPS):
+                            act(to, c)
         for i in range(1, GROUPS):
             act(wa, lax.rem(ch + i, GROUPS))
 
-        def several(d, carry):
-            other = lax.rem(wa + d, LAYERS)
-            for c in range(GROUPS):
-                act(other, c)
-            return carry
-
-        lax.fori_loop(1, LAYERS, several, 0)
-
     def greet(w, c):
         pl.semaphore_signal(barrier, inc=1, device_id=(w, c), device_id_type=mesh_id)
 
     each_peer(greet)
+    for load in loads:
+        load.wait()
     mydepth[0] = jnp.zeros((1, LANES), F32) + depth[0]
     fill_blocks(cells, vis, weights, layer, group, blocks, notes)
     sub = lax.broadcasted_iota(I32, (8, LANES), 0)
@@ -155,12 +179,10 @@
     acc[...] = jnp.zeros_like(acc)
     pl.semaphore_wait(barrier, ALL)
 
-    x, zy = wa // 8, lax.rem(wa, 8)
-    z, y = zy // 4, lax.rem(zy, 4)
     for i, (dx, dz) in enumerate(STAGES):
         for dy in range(4):
             if dx or dz or dy:
-                to = lax.rem(x + dx, 4) * 8 + lax.rem(z + dz, 2) * 4 + lax.rem(y + dy, 4)
+                to = moved(dx, dz, dy)
                 pltpu.make_async_remote_copy(
                     src_ref=mydepth.at[0], dst_ref=depths.at[wa],
                     send_sem=depth_send, recv_sem=depth_recv.at[i],
@@ -220,20 +242,27 @@
 
         w = cmul((zr, zi), sincos_phase((2 * row0 + 1551) * u - 1793 * v))
         step = sincos_phase(512 * v)
-        for c0 in range(BLOCKS):
+        last, w = w, cmul(w, step)
+        put(wtab, 32, 0, last[0])
+        put(wtab, 32, 1, last[1])
+        twice = step[0] + step[0]
+        for c0 in range(1, BLOCKS):
             put(wtab, 32, c0 * 2, w[0])
             put(wtab, 32, c0 * 2 + 1, w[1])
             if c0 + 1 < BLOCKS:
-                w = cmul(w, step)
+                last, w = w, (twice * w[0] - last[0], twice * w[1] - last[1])
         e = sincos_phase(u)
-        step = csquare(e)
+        last = e[0], -e[1]
+        twice = 2.0 - 4.0 * (e[1] * e[1])
         for n in range(8):
             put(ltab, 16, n, e[0])
             put(ltab, 16, 8 + n, e[1])
             if n < 7:
-                e = cmul(e, step)
+                last, e = e, (twice * e[0] - last[0], twice * e[1] - last[1])
         e = sincos_phase(v)
         step = csquare(e)
+        last = e[0], -e[1]
+        twice = step[0] + step[0]
         eighth = csquare(csquare(csquare(step)))
         for n in range(8):
             put(ntab, 32, n, e[0])
@@ -241,7 +270,7 @@
             put(ntab, 32, 16 + n, e[1])
             put(ntab, 32, 31 - n, e[1])
             if n < 7:
-                e = cmul(e, step)
+                last, e = e, (twice * e[0] - last[0], twice * e[1] - last[1])
         c8[pl.ds(base, 32), :] = 2.0 * eighth[0]
         return carry
 
@@ -337,10 +366,10 @@
                 tile = jnp.take_along_axis(tile, back_lane, axis=1, mode="promise_in_bounds")
             cols = slice(c0 * 256 + (128 if k % 2 == 0 else 0), c0 * 256 + (256 if k % 2 == 0 else 128))
             if k < 2:
-                out[8:16, cols] = tile - sky[8:16, cols]
+                out[8:16, cols] = tile
             else:
                 for n in range(8):
-                    out[7 - n : 8 - n, cols] = tile[n : n + 1] - sky[7 - n : 8 - n, cols]
+                    out[7 - n : 8 - n, cols] = tile[n : n + 1]
     pltpu.make_async_copy(all_notes, all_notes, note_send).wait()
     others = depths.at[pl.ds(0, LAYERS - 1)]
     pltpu.make_async_copy(others, others, depth_send).wait()
@@ -351,13 +380,20 @@
 
 def on_device(grid_cells, visibilities, weights, layer_index, group_index, plane_depths, sky_model):
     vmem = pl.BlockSpec(memory_space=pltpu.VMEM)
-    smem = pl.BlockSpec(memory_space=pltpu.SMEM)
-    residual = pl.pallas_call(
+    hbm = pl.BlockSpec(memory_space=pltpu.HBM)
+    dirty = pl.pallas_call(
         kernel,
         out_shape=jax.ShapeDtypeStruct((ROWS, COLS), F32),
-        in_specs=[vmem] * 5 + [smem, vmem],
+        in_specs=[hbm] * 6,
         out_specs=vmem,
         scratch_shapes=[
+            pltpu.VMEM((2, VIS_DEV), I32),
+            pltpu.VMEM((2, VIS_DEV), F32),
+            pltpu.VMEM((1, VIS_DEV), F32),
+            pltpu.VMEM((1, VIS_DEV), I32),
+            pltpu.VMEM((1, VIS_DEV), I32),
+            pltpu.SMEM((1,), F32),
+            pltpu.SemaphoreType.DMA((6,)),
             pltpu.VMEM((GROUPS, 2, 4, LANES), F32),
             pltpu.VMEM((GROUPS, 1, LANES), F32),
             pltpu.VMEM((2, SOURCES, 4, LANES), F32),
@@ -393,9 +429,8 @@
         layer_index.reshape(1, VIS_DEV),
         group_index.reshape(1, VIS_DEV),
         plane_depths,
-        sky_model[0],
     )
-    return residual[None]
+    return dirty[None] - sky_model
 
 
 def solution(mesh):

time: 39.4 us -> 36.7 us (0.931)
  Pallas kernels: 36.9 us -> 34.2 us
  other arithmetic: 0 us -> 1.68 us
  local copies, waits for them, and re-layouts: 1.67 us -> 0.01 us
    pallas_call x1, Pallas kernels: 36.9 us -> 34.2 us  [on_device(): pl.pallas_call(kernel, out_shape=jax.ShapeDtypeStruct((ROWS, COLS), F32),...]
    sub x0 -> x1, other arithmetic: none -> 1.68 us  [on_device(): return dirty[None] - sky_model]
    unnamed x1 -> x2, local copies, waits for them, and re-layouts: 1.67 us -> 0.01 us
where the time goes in v6:
time: 36.7 us; the launch traced here: 36.6 us
  Pallas kernels  34.2 us (93%)
  other arithmetic  1.68 us (5%)
  between operations  0.71 us (2%)
    pallas_call x1, Pallas kernels, on_device(): pl.pallas_call(kernel, out_shape=jax.ShapeDtypeStruct((ROWS, COLS), F32),...  34.2 us
    sub x1, other arithmetic, on_device(): return dirty[None] - sky_model  1.68 us

profile of v6, /device:TPU:1, one launch (start us, length us, event | category | flops | bytes accessed | tf_op | source)
XLA Modules:
  0.0 36.6 jit_solution(1254611574633976368)
XLA Ops:
  0.0 0.0 copy-start
  0.7 34.2 %cycle.1 = f32[16,4096]{1,0:T(8,128)} custom-call(s32[2,512]{1,0:T(2,128)} %cells_hbm.1, f32[2,512]{1,0:T(2,128)} %vis_hbm.1, f32[1,512]{1,0:T(1,128)} %bitcast.5, s32[1,512]{1,0:T(1,128)} %bitcast.6, s32[1,512]{1,0:T(1,128)} %bitcast.7, f32[1]{0:T(128)S(6)} %copy.8.depth_hbm), custom_call_target="tpu_custom_call" | custom-call | tf_op jit(solution)/shard_map/cycle/pallas_call | solution.py:384
  34.9 0.0 copy-done
  34.9 1.7 %bitcast_subtract_fusion = f32[1,16,4096]{2,1,0:T(8,128)} fusion(f32[1,16,4096]{2,1,0:T(8,128)S(1)} %copy-done, f32[16,4096]{1,0:T(8,128)} %cycle.1), kind=kLoop, calls=%fused_computation | loop fusion | flops 65536 | bytes 786432 | tf_op jit(solution)/shard_map/sub | solution.py:433
Async XLA Ops:
  0.0 34.9 %copy-start = (f32[1,16,4096]{2,1,0:T(8,128)S(1)}, f32[1,16,4096]{2,1,0:T(8,128)}, u32[]{:S(2)}) copy-start(f32[1,16,4096]{2,1,0:T(8,128)} %param.13) | copy-start | bytes 786436

commit v7 on v6

--- a/solution.py
+++ b/solution.py
@@ -26,7 +26,7 @@
 FAR_FIRST = (2, 1, 3, 0)
 STAGES = ((0, 0), (0, 1), (1, 0), (3, 0), (1, 1), (3, 1), (2, 0), (2, 1))
 
-SIN_C = (4.442882919124344, -7.308245686509099, 3.6063542184331383, -0.8461116503741475, 0.10982451642439378)
+SIN_C = (4.442867903034145, -7.307443421379447, 3.5947880792825875, -0.7843740327506916)
 COS_C = (1.4142134962552289, -6.978850948563853, 5.7394603769076955, -1.8835579059892091, 0.31068802753070307)
 
 
@@ -177,6 +177,7 @@
                 t = (c0 * 2 + sl) * 2 + sn
                 dterm[t * 8 : t * 8 + 8, :] = -q / (1.0 + jnp.sqrt(1.0 - q))
     acc[...] = jnp.zeros_like(acc)
+    x_b[...] = jnp.zeros_like(x_b)
     pl.semaphore_wait(barrier, ALL)
 
     for i, (dx, dz) in enumerate(STAGES):
@@ -326,24 +327,24 @@
         arrive(0)
         tables(0, 0)
         expand(0, lhs_a, rhs_a)
-        multiply(x_a, lhs_a, rhs_a)
-        expand(1, lhs_b, rhs_b)
 
         def several(jj, carry):
-            tables(jnp.minimum(jj + 1, LAYERS // 4 - 1), 0)
             for i in range(0, 4, 2):
                 j = 4 * jj + i
+                multiply(x_a, lhs_a, rhs_a)
+                if i == 0:
+                    tables(jnp.minimum(jj + 1, LAYERS // 4 - 1), 0)
+                image(jnp.maximum(j - 1, 0), x_b)
+                expand(j + 1, lhs_b, rhs_b)
                 multiply(x_b, lhs_b, rhs_b)
                 image(j, x_a)
                 expand(jnp.minimum(j + 2, LAYERS - 1), lhs_a, rhs_a)
-                multiply(x_a, lhs_a, rhs_a)
-                image(j + 1, x_b)
-                expand(jnp.minimum(j + 3, LAYERS - 1), lhs_b, rhs_b)
             return carry
 
         lax.fori_loop(0, LAYERS // 8 - 1, several, 0)
         arrive(1)
         lax.fori_loop(LAYERS // 8 - 1, LAYERS // 4, several, 0)
+        image(LAYERS - 1, x_b)
 
     pl.run_scoped(
         all_layers,

time: 36.7 us -> 35.7 us (0.973)
  Pallas kernels: 34.2 us -> 33.2 us
    pallas_call x1, Pallas kernels: 34.2 us -> 33.2 us  [on_device(): pl.pallas_call(kernel, out_shape=jax.ShapeDtypeStruct((ROWS, COLS), F32),...]
where the time goes in v7:
time: 35.7 us; the launch traced here: 35.5 us
  Pallas kernels  33.2 us (93%)
  other arithmetic  1.68 us (5%)
  between operations  0.71 us (2%)
    pallas_call x1, Pallas kernels, on_device(): pl.pallas_call(kernel, out_shape=jax.ShapeDtypeStruct((ROWS, COLS), F32),...  33.2 us
    sub x1, other arithmetic, on_device(): return dirty[None] - sky_model  1.68 us

profile of v7, /device:TPU:1, one launch (start us, length us, event | category | flops | bytes accessed | tf_op | source)
XLA Modules:
  0.0 35.5 jit_solution(10807443350752428691)
XLA Ops:
  0.0 0.0 copy-start
  0.7 33.2 %cycle.1 = f32[16,4096]{1,0:T(8,128)} custom-call(s32[2,512]{1,0:T(2,128)} %cells_hbm.1, f32[2,512]{1,0:T(2,128)} %vis_hbm.1, f32[1,512]{1,0:T(1,128)} %bitcast.5, s32[1,512]{1,0:T(1,128)} %bitcast.6, s32[1,512]{1,0:T(1,128)} %bitcast.7, f32[1]{0:T(128)S(6)} %copy.8.depth_hbm), custom_call_target="tpu_custom_call" | custom-call | tf_op jit(solution)/shard_map/cycle/pallas_call | solution.py:385
  33.9 0.0 copy-done
  33.9 1.7 %bitcast_subtract_fusion = f32[1,16,4096]{2,1,0:T(8,128)} fusion(f32[1,16,4096]{2,1,0:T(8,128)S(1)} %copy-done, f32[16,4096]{1,0:T(8,128)} %cycle.1), kind=kLoop, calls=%fused_computation | loop fusion | flops 65536 | bytes 786432 | tf_op jit(solution)/shard_map/sub | solution.py:434
Async XLA Ops:
  0.0 33.9 %copy-start = (f32[1,16,4096]{2,1,0:T(8,128)S(1)}, f32[1,16,4096]{2,1,0:T(8,128)}, u32[]{:S(2)}) copy-start(f32[1,16,4096]{2,1,0:T(8,128)} %param.13) | copy-start | bytes 786436

commit v8 on v7

--- a/solution.py
+++ b/solution.py
@@ -24,7 +24,9 @@
 BLOCKS = COLS // 256
 ALL = SOURCES - 1
 FAR_FIRST = (2, 1, 3, 0)
-STAGES = ((0, 0), (0, 1), (1, 0), (3, 0), (1, 1), (3, 1), (2, 0), (2, 1))
+HOPS = (0, 1, 2, 1)
+OFFSETS = [(dx, dz, dy) for dx in range(4) for dz in range(2) for dy in range(4)]
+CLASSES = [[o for o in OFFSETS if HOPS[o[0]] + o[1] + HOPS[o[2]] == h] for h in range(6)]
 
 SIN_C = (4.442867903034145, -7.307443421379447, 3.5947880792825875, -0.7843740327506916)
 COS_C = (1.4142134962552289, -6.978850948563853, 5.7394603769076955, -1.8835579059892091, 0.31068802753070307)
@@ -164,6 +166,39 @@
         load.wait()
     mydepth[0] = jnp.zeros((1, LANES), F32) + depth[0]
     fill_blocks(cells, vis, weights, layer, group, blocks, notes)
+    pl.semaphore_wait(barrier, ALL)
+
+    for i, offsets in enumerate(CLASSES):
+        for dx, dz, dy in offsets:
+            if i:
+                pltpu.make_async_remote_copy(
+                    src_ref=mydepth.at[0], dst_ref=depths.at[wa],
+                    send_sem=depth_send, recv_sem=depth_recv.at[i],
+                    device_id=(moved(dx, dz, dy), lax.rem(ch + 2 * dz, GROUPS)), device_id_type=mesh_id,
+                ).start()
+    for half in range(2):
+
+        def send(w, c):
+            pltpu.make_async_remote_copy(
+                src_ref=blocks.at[c, half], dst_ref=recv.at[half, me],
+                send_sem=send_sem.at[half], recv_sem=recv_sem.at[half],
+                device_id=(w, c), device_id_type=mesh_id,
+            ).start()
+
+        each_peer(send)
+
+    def send_note(w, c):
+        pltpu.make_async_remote_copy(
+            src_ref=notes.at[c], dst_ref=heard.at[me], send_sem=note_send, recv_sem=note_recv,
+            device_id=(w, c), device_id_type=mesh_id,
+        ).start()
+
+    each_peer(send_note)
+    for half in range(2):
+        recv[half, me] = blocks[ch, half]
+    heard[me] = notes[ch]
+    depths[wa] = mydepth[0]
+
     sub = lax.broadcasted_iota(I32, (8, LANES), 0)
     lane = lax.broadcasted_iota(I32, (8, LANES), 1)
     for sl in range(2):
@@ -178,56 +213,25 @@
                 dterm[t * 8 : t * 8 + 8, :] = -q / (1.0 + jnp.sqrt(1.0 - q))
     acc[...] = jnp.zeros_like(acc)
     x_b[...] = jnp.zeros_like(x_b)
-    pl.semaphore_wait(barrier, ALL)
-
-    for i, (dx, dz) in enumerate(STAGES):
-        for dy in range(4):
-            if dx or dz or dy:
-                to = moved(dx, dz, dy)
-                pltpu.make_async_remote_copy(
-                    src_ref=mydepth.at[0], dst_ref=depths.at[wa],
-                    send_sem=depth_send, recv_sem=depth_recv.at[i],
-                    device_id=(to, lax.rem(ch + 2 * dz, GROUPS)), device_id_type=mesh_id,
-                ).start()
-    for half in range(2):
-
-        def send(w, c):
-            pltpu.make_async_remote_copy(
-                src_ref=blocks.at[c, half], dst_ref=recv.at[half, me],
-                send_sem=send_sem.at[half], recv_sem=recv_sem.at[half],
-                device_id=(w, c), device_id_type=mesh_id,
-            ).start()
-
-        each_peer(send)
-
-    def send_note(w, c):
-        pltpu.make_async_remote_copy(
-            src_ref=notes.at[c], dst_ref=heard.at[me], send_sem=note_send, recv_sem=note_recv,
-            device_id=(w, c), device_id_type=mesh_id,
-        ).start()
-
-    each_peer(send_note)
-    for half in range(2):
-        recv[half, me] = blocks[ch, half]
-    heard[me] = notes[ch]
-    depths[wa] = mydepth[0]
-
-    for i, (dx, dz) in enumerate(STAGES):
-        some = depths.at[pl.ds(0, 4 if i else 3)]
-        pltpu.make_async_copy(some, some, depth_recv.at[i]).wait()
-        first = lax.rem(x + (4 - dx), 4) * 8 + lax.rem(z + dz, 2) * 4
-
-        def screens(n, carry):
-            j = first + n
-            w = depths[j]
-            for p in range(64):
-                t = w * dterm[p * 8 : p * 8 + 8, :]
-                s, c = half_turns(t - jnp.round(t))
-                stab[j, p * 8 : p * 8 + 8, :] = s
-                ctab[j, p * 8 : p * 8 + 8, :] = c
-            return carry
-
-        lax.fori_loop(0, 4, screens, 0)
+    def screens(n, codes):
+        dx, dz, dy = lax.rem(codes // 8, 4), lax.rem(codes // 4, 2), lax.rem(codes, 4)
+        j = lax.rem(x + 4 - dx, 4) * 8 + lax.rem(z + dz, 2) * 4 + lax.rem(y + 4 - dy, 4)
+        w = depths[j]
+        for p in range(64):
+            t = w * dterm[p * 8 : p * 8 + 8, :]
+            s, c = half_turns(t - jnp.round(t))
+            stab[j, p * 8 : p * 8 + 8, :] = s
+            ctab[j, p * 8 : p * 8 + 8, :] = c
+        return codes // 32
+
+    for i, offsets in enumerate(CLASSES):
+        if i:
+            some = depths.at[pl.ds(0, len(offsets))]
+            pltpu.make_async_copy(some, some, depth_recv.at[i]).wait()
+        for at in range(0, len(offsets), 5):
+            part = offsets[at : at + 5]
+            codes = sum((dx * 8 + dz * 4 + dy) * 32**k for k, (dx, dz, dy) in enumerate(part))
+            lax.fori_loop(0, len(part), screens, jnp.int32(codes))
 
     def tables(jc, carry):
         base = pl.multiple_of(jc * 32, 32)
@@ -417,7 +421,7 @@
             pltpu.SemaphoreType.DMA,
             pltpu.SemaphoreType.DMA,
             pltpu.SemaphoreType.DMA,
-            pltpu.SemaphoreType.DMA((len(STAGES),)),
+            pltpu.SemaphoreType.DMA((len(CLASSES),)),
         ],
         compiler_params=pltpu.CompilerParams(
             collective_id=0, has_side_effects=True, vmem_limit_bytes=60 * 1024 * 1024

time: 35.7 us -> 36.3 us (1.017)
  Pallas kernels: 33.2 us -> 33.8 us
    pallas_call x1, Pallas kernels: 33.2 us -> 33.8 us  [on_device(): pl.pallas_call(kernel, out_shape=jax.ShapeDtypeStruct((ROWS, COLS), F32),...]
where the time goes in v8:
time: 36.3 us; the launch traced here: 36.2 us
  Pallas kernels  33.8 us (93%)
  other arithmetic  1.68 us (5%)
  between operations  0.71 us (2%)
    pallas_call x1, Pallas kernels, on_device(): pl.pallas_call(kernel, out_shape=jax.ShapeDtypeStruct((ROWS, COLS), F32),...  33.8 us
    sub x1, other arithmetic, on_device(): return dirty[None] - sky_model  1.68 us

profile of v8, /device:TPU:1, one launch (start us, length us, event | category | flops | bytes accessed | tf_op | source)
XLA Modules:
  0.0 36.2 jit_solution(18384286757047495388)
XLA Ops:
  0.0 0.0 copy-start
  0.7 33.8 %cycle.1 = f32[16,4096]{1,0:T(8,128)} custom-call(s32[2,512]{1,0:T(2,128)} %cells_hbm.1, f32[2,512]{1,0:T(2,128)} %vis_hbm.1, f32[1,512]{1,0:T(1,128)} %bitcast.5, s32[1,512]{1,0:T(1,128)} %bitcast.6, s32[1,512]{1,0:T(1,128)} %bitcast.7, f32[1]{0:T(128)S(6)} %copy.8.depth_hbm), custom_call_target="tpu_custom_call" | custom-call | tf_op jit(solution)/shard_map/cycle/pallas_call | solution.py:389
  34.5 0.0 copy-done
  34.5 1.7 %bitcast_subtract_fusion = f32[1,16,4096]{2,1,0:T(8,128)} fusion(f32[1,16,4096]{2,1,0:T(8,128)S(1)} %copy-done, f32[16,4096]{1,0:T(8,128)} %cycle.1), kind=kLoop, calls=%fused_computation | loop fusion | flops 65536 | bytes 786432 | tf_op jit(solution)/shard_map/sub | solution.py:438
Async XLA Ops:
  0.0 34.5 %copy-start = (f32[1,16,4096]{2,1,0:T(8,128)S(1)}, f32[1,16,4096]{2,1,0:T(8,128)}, u32[]{:S(2)}) copy-start(f32[1,16,4096]{2,1,0:T(8,128)} %param.13) | copy-start | bytes 786436
